TPU v7x, 32 devices: a whole 2x2x4 slice. The times are simulated.
32 devices in a mesh: ctx: 2 (over x), tp: 4 (over y, core), dp: 4 (over z).
Axes of the slice: x: 2, y: 2, z: 4, core: 2. Of those that a mesh axis runs over, the one named last changes fastest.
Arguments:
- hidden: bfloat16 [4, 1024, 4096], P('dp', 'ctx', 'tp'), may hold values from -6 to 6
- target: bfloat16 [4, 1024, 4096], P('dp', 'ctx', 'tp'), may hold values from -24 to 24
- gain: float32 [4096], replicated, may hold values from 0.5 to 1.5
- w_query: bfloat16 [4096, 2048], P(('ctx', 'dp'), 'tp'), may hold values from -2.15625 to 2.15625
- w_key: bfloat16 [4096, 512], P(('ctx', 'dp'), 'tp'), may hold values from -0.09375 to 0.09375
- value_matrix: bfloat16 [4096, 512], P(('ctx', 'dp'), 'tp'), may hold values from -0.09375 to 0.09375
- w_out: bfloat16 [2048, 4096], P('tp', ('ctx', 'dp')), may hold values from -0.125 to 0.125
- block_order: int32 [4], replicated, may hold values from 0 to 3, each once
Outputs:
- branch: bfloat16 [4, 1024, 4096], P('dp', 'ctx', 'tp')
- loss: float32 [], replicated
Inputs may be any that keep to these rules, and one draw needn't show every extreme that they name: block_order is a permutation of 0 to 3.
All inputs are finite; a program needn't handle non-finite values.
Results may differ from a plain program's by a relative error of at most 0.013.
The roundings to bfloat16 on the way count: a program that leaves them out, or rounds other values in their place, can miss the bound.
Values may be sent and summed in bfloat16 or wider, within the bound.
A program may use at most 128 MiB of HBM per device.

v0:
```python
import functools

import jax
import jax.numpy as jnp
from jax import lax
from jax.experimental import pallas as pl
from jax.experimental.pallas import tpu as pltpu
from jax.sharding import PartitionSpec as P

MODEL_WIDTH = 4096
QUERY_HEADS = 16
KEY_VALUE_HEADS = 4
HEAD_SIZE = 128


rope_base = 500000.0


def shifted(value, axis, by):
    peers = lax.axis_size(axis)
    return lax.ppermute(value, axis, [(i, (i + by) % peers) for i in range(peers)])


def positions(order, start, rows, half):
    index = start + lax.iota(jnp.int32, rows)
    block = index // half
    slots = lax.iota(jnp.int32, order.shape[0])
    chosen = jnp.sum(jnp.where(block[:, None] == slots[None, :], order[None, :], 0), axis=1)
    return chosen * half + index % half


def apply_rotary(values, token_places):
    half = values.shape[-1] // 2
    freqs = rope_base ** (-(jnp.arange(half, dtype=jnp.float32) * 2.0) / values.shape[-1])
    angles = token_places.astype(jnp.float32)[:, None] * freqs[None, :]
    cosine = jnp.cos(angles)[:, None, :]
    sine = jnp.sin(angles)[:, None, :]
    first = values[..., :half]
    second = values[..., half:]
    return jnp.concatenate(
        [first * cosine - second * sine, second * cosine + first * sine], axis=-1
    )


def attend(state, query_rows, qpos, piece, kpos):
    peak, total, accum = state
    rows = piece.shape[1]
    local_heads = query_rows.shape[1]
    pair = piece.reshape(2, rows, local_heads, HEAD_SIZE)
    scores = jnp.einsum(
        "qcgd,kcd->cgqk", query_rows, pair[0], preferred_element_type=jnp.float32
    ) * (1.0 / HEAD_SIZE**0.5)
    allowed = (qpos[:, None] >= kpos[None, :])[None, None]
    scores = jnp.where(allowed, scores, -1e30)
    new_peak = jnp.maximum(peak, jnp.max(scores, axis=-1))
    weights = jnp.where(allowed, jnp.exp(scores - new_peak[..., None]), 0.0)
    factor = jnp.exp(peak - new_peak)
    total = total * factor + jnp.sum(weights, axis=-1)
    update = jnp.einsum(
        "cgqk,kcd->qcgd", weights.astype(jnp.bfloat16), pair[1], preferred_element_type=jnp.float32
    )
    accum = accum * jnp.transpose(factor, (2, 0, 1))[..., None] + update
    return (new_peak, total, accum)


def on_device(hidden, target, gain, w_query, w_key, value_matrix, w_out, block_order):
    rows = hidden.shape[1]
    half = rows // 2
    local = hidden[0]
    whole = lax.all_gather(local, "tp", axis=1, tiled=True)
    wide = whole.astype(jnp.float32)
    normed = (
        wide * lax.rsqrt(jnp.mean(wide * wide, axis=1, keepdims=True) + 1e-05) * gain[None, :]
    ).astype(jnp.bfloat16)
    pieces = (
        lax.all_gather(w_query, ("ctx", "dp"), axis=0, tiled=True),
        lax.all_gather(w_key, ("ctx", "dp"), axis=0, tiled=True),
        lax.all_gather(value_matrix, ("ctx", "dp"), axis=0, tiled=True),
    )
    query_rows, key, value_rows = tuple(
        (jnp.dot(normed, piece, preferred_element_type=jnp.float32) for piece in pieces)
    )
    shard = lax.axis_index("ctx")
    qpos = positions(block_order, shard * rows, rows, half)
    local_heads = w_key.shape[1] // HEAD_SIZE
    query_group = QUERY_HEADS // KEY_VALUE_HEADS
    query_rows = (
        apply_rotary(query_rows.reshape(rows, local_heads * query_group, HEAD_SIZE), qpos)
        .astype(jnp.bfloat16)
        .reshape(rows, local_heads, query_group, HEAD_SIZE)
    )
    key = (
        apply_rotary(key.reshape(rows, local_heads, HEAD_SIZE), qpos)
        .astype(jnp.bfloat16)
        .reshape(rows, local_heads * HEAD_SIZE)
    )
    pair = jnp.stack([key, value_rows.astype(jnp.bfloat16)])
    state = (
        jnp.full((local_heads, query_group, rows), -1e30, jnp.float32),
        jnp.zeros((local_heads, query_group, rows), jnp.float32),
        jnp.zeros((rows, local_heads, query_group, HEAD_SIZE), jnp.float32),
    )
    count = lax.axis_size("ctx")
    state = attend(state, query_rows, qpos, pair, qpos)

    def turn(step, carry):
        moved, inner = carry
        moved = shifted(moved, "ctx", 1)
        source = (shard - step) % count
        return (
            moved,
            attend(
                inner, query_rows, qpos, moved, positions(block_order, source * rows, rows, half)
            ),
        )

    moved_end, state = lax.fori_loop(1, count, turn, (pair, state))
    peak, total, accum = state
    attn = (
        (accum / jnp.transpose(total, (2, 0, 1))[..., None])
        .astype(jnp.bfloat16)
        .reshape(rows, local_heads * query_group * HEAD_SIZE)
    )
    terms = jnp.dot(
        attn,
        lax.all_gather(w_out, ("ctx", "dp"), axis=1, tiled=True),
        preferred_element_type=jnp.float32,
    )
    summed = lax.psum_scatter(terms.astype(jnp.bfloat16), "tp", scatter_dimension=1, tiled=True)
    resid = local.astype(jnp.float32) + summed.astype(jnp.float32) - target[0].astype(jnp.float32)
    squares = lax.psum(jnp.sum(resid * resid), ("ctx", "tp", "dp"))
    loss = squares / (lax.axis_size("dp") * lax.axis_size("ctx") * rows * MODEL_WIDTH)
    return (summed[None], loss)


MESH = pl.DeviceIdType.MESH
F32 = jnp.float32
BF16 = jnp.bfloat16


def layer(
    nd,
    order,
    hidden,
    target,
    gain,
    freqs,
    w_query,
    w_key,
    value_matrix,
    w_out,
    out,
    loss,
    ga,
    go,
    xs,
    goal,
    normed,
    acc,
    trig,
    query,
    kv,
    attn,
    kept,
    sent,
    sib,
    ysend,
    yrecv,
    tile,
    sums_tp,
    sums_all,
    load_sem,
    a_send,
    a_recv,
    o_send,
    o_recv,
    h_send,
    h_recv,
    kv_send,
    kv_recv,
    s_send,
    s_recv,
    y_send,
    y_recv,
    t_send,
    t_recv,
    l_send,
    l_recv,
):
    c, t, d = lax.axis_index("ctx"), lax.axis_index("tp"), lax.axis_index("dp")
    nb = 2 * nd
    me = c * nd + d
    y, k = t // 2, t % 2
    sibling = y * 2 + (1 - k)
    across = (1 - y) * 2 + k
    diagonal = (1 - y) * 2 + (1 - k)
    rows, wide = hidden.shape
    deep = w_query.shape[0]
    qcols = w_query.shape[1]
    half = rows // 2
    n_heads = qcols // HEAD_SIZE
    e = d + 1 - 2 * (d % 2)

    loads = [
        pltpu.make_async_copy(w_query, ga.at[me, :, pl.ds(0, qcols)], load_sem.at[0]),
        pltpu.make_async_copy(w_key, ga.at[me, :, pl.ds(qcols, HEAD_SIZE)], load_sem.at[1]),
        pltpu.make_async_copy(
            value_matrix, ga.at[me, :, pl.ds(qcols + HEAD_SIZE, HEAD_SIZE)], load_sem.at[2]
        ),
        pltpu.make_async_copy(hidden, xs.at[t], load_sem.at[3]),
        pltpu.make_async_copy(w_out, go.at[me], load_sem.at[4]),
        pltpu.make_async_copy(target, goal, load_sem.at[5]),
    ]
    for load in loads:
        load.start()

    barrier = pltpu.get_barrier_semaphore()
    for s in range(1, nb):
        p = (me + s) % nb
        pl.semaphore_signal(
            barrier, inc=1, device_id={"ctx": p // nd, "dp": p % nd}, device_id_type=MESH
        )
    for s in (sibling, across, diagonal):
        pl.semaphore_signal(barrier, inc=1, device_id={"tp": s}, device_id_type=MESH)
    pl.semaphore_wait(barrier, nb + 2)

    def remote(src, dst, ssem, rsem, where):
        return pltpu.make_async_remote_copy(
            src_ref=src, dst_ref=dst, send_sem=ssem, recv_sem=rsem,
            device_id=where, device_id_type=MESH,
        )

    X, UP, DOWN = 0, 1, 2

    def piece(buf, ssem, rsem, b, way):
        where = {
            X: {"ctx": 1 - c},
            UP: {"dp": jnp.minimum(d + 1, nd - 1)},
            DOWN: {"dp": jnp.maximum(d - 1, 0)},
        }[way]
        return remote(buf.at[b], buf.at[b], ssem.at[way, b], rsem.at[b], where)

    def a_piece(b, way):
        return piece(ga, a_send, a_recv, b, way)

    def o_piece(b, way):
        return piece(go, o_send, o_recv, b, way)

    def block(src, j, dst, i, ssem, rsem, where):
        return remote(src.at[j], dst.at[i], ssem, rsem, {"tp": where})

    def h_copy(slot, i, where):
        return block(xs, slot, xs, slot, h_send.at[i], h_recv.at[i], where)

    h_sib = h_copy(t, 0, sibling)
    h_across = h_copy(t, 1, across)
    h_relay = h_copy(across, 2, sibling)
    for i in range(3):
        loads[i].wait()
    a_piece(me, X).start()
    up, down = d < nd - 1, d > 0

    @pl.when(up)
    def _():
        a_piece(me, UP).start()

    @pl.when(down)
    def _():
        a_piece(me, DOWN).start()

    loads[3].wait()
    h_across.start()
    h_sib.start()
    loads[4].wait()
    loads[5].wait()

    def positions_of(shard, index):
        low = order[2 * shard] * half
        high = order[2 * shard + 1] * half
        return jnp.where(index < half, low + index, high + index - half)

    place = positions_of(c, lax.broadcasted_iota(jnp.int32, (rows, HEAD_SIZE), 0)).astype(F32)
    angle = place * freqs[...]
    lane = lax.broadcasted_iota(jnp.int32, (rows, HEAD_SIZE), 1)
    trig[0] = jnp.cos(angle)
    sine = jnp.sin(angle)
    trig[1] = jnp.where(lane < HEAD_SIZE // 2, -sine, sine)

    def relay_a(s):
        @pl.when(d >= s)
        def _():
            b = me - s
            a_piece(b, DOWN).wait_recv()
            a_piece(b, X).start()

            @pl.when(up)
            def _():
                a_piece(b, UP).start()

        @pl.when(d + s < nd)
        def _():
            b = me + s
            a_piece(b, UP).wait_recv()
            a_piece(b, X).start()

            @pl.when(down)
            def _():
                a_piece(b, DOWN).start()

    relay_a(1)

    h_copy(across, 1, across).wait_recv()
    h_relay.start()
    h_copy(sibling, 0, sibling).wait_recv()
    h_copy(diagonal, 2, sibling).wait_recv()
    tp = xs.shape[0]
    chunk = 64
    per = wide // deep

    def norm_rows(i, carry):
        r = pl.multiple_of(i * chunk, chunk)
        total = jnp.zeros((chunk, 1), F32)
        for j in range(tp):
            v = xs[j, pl.ds(r, chunk), :].astype(F32)
            total = total + jnp.sum(v * v, axis=1, keepdims=True)
        scale = lax.rsqrt(total * (1.0 / (tp * wide)) + 1e-05)
        for j in range(tp):
            for m in range(per):
                v = xs[j, pl.ds(r, chunk), m * deep : (m + 1) * deep].astype(F32)
                g = gain[:, j * wide + m * deep : j * wide + (m + 1) * deep]
                normed[j * per + m, pl.ds(r, chunk), :] = (v * scale * g).astype(BF16)
        return carry

    lax.fori_loop(0, rows // chunk, norm_rows, 0)

    for s in range(2, nd):
        relay_a(s)
        if s == nd - 2:

            @pl.when(up)
            def _():
                o_piece(me, UP).start()

            @pl.when(down)
            def _():
                o_piece(me, DOWN).start()

    acc[...] = jnp.zeros_like(acc)

    def project(b):
        acc[...] += jnp.dot(normed[b], ga[b], preferred_element_type=F32)

    def own_line(i, carry):
        project(c * nd + i)
        return carry

    lax.fori_loop(0, nd, own_line, 0)

    def relay_o_line(s):
        @pl.when(d >= s)
        def _():
            b = me - s
            o_piece(b, DOWN).wait_recv()

            @pl.when(up)
            def _():
                o_piece(b, UP).start()

        @pl.when(d + s < nd)
        def _():
            b = me + s
            o_piece(b, UP).wait_recv()

            @pl.when(down)
            def _():
                o_piece(b, DOWN).start()

    def relay_o_x(s):
        @pl.when((d >= s) & (d - s != e))
        def _():
            o_piece(me - s, X).start()

        @pl.when((d + s < nd) & (d + s != e))
        def _():
            o_piece(me + s, X).start()

    relay_o_line(1)

    def other_line(i, carry):
        far = jnp.where(d < nd // 2, i, nd - 1 - i)
        b = (1 - c) * nd + far
        a_piece(b, X).wait_recv()
        project(b)
        return carry

    lax.fori_loop(0, nd, other_line, 0)

    def rotated(v):
        return (v * trig[0] + pltpu.roll(v, HEAD_SIZE // 2, 1) * trig[1]).astype(BF16)

    kv[c, :, 0:HEAD_SIZE] = rotated(acc[:, qcols : qcols + HEAD_SIZE])
    kv[c, :, HEAD_SIZE:] = acc[:, qcols + HEAD_SIZE :].astype(BF16)
    kv_copy = remote(kv.at[c], kv.at[c], kv_send.at[0], kv_recv.at[0], {"ctx": 1 - c})
    kv_copy.start()
    o_piece(me, X).start()
    relay_o_x(1)
    for h in range(n_heads):
        part = slice(h * HEAD_SIZE, (h + 1) * HEAD_SIZE)
        query[h] = rotated(acc[:, part])
    for s in range(2, nd - 1):
        relay_o_line(s)
        relay_o_x(s)

    remote(kv.at[1 - c], kv.at[1 - c], kv_send.at[0], kv_recv.at[0], {"ctx": 1 - c}).wait_recv()
    qrows = 256
    dims = (((1,), (1,)), ((), ()))

    def attend_block(i, carry):
        h = i // (rows // qrows)
        r = pl.multiple_of((i % (rows // qrows)) * qrows, qrows)
        q = query[h, pl.ds(r, qrows), :]
        qpos = positions_of(c, r + lax.broadcasted_iota(jnp.int32, (qrows, rows), 0))
        scores = []
        for n in range(2):
            kpos = positions_of(n, lax.broadcasted_iota(jnp.int32, (qrows, rows), 1))
            sc = lax.dot_general(
                q, kv[n, :, 0:HEAD_SIZE], dims, preferred_element_type=F32
            ) * (1.0 / HEAD_SIZE**0.5)
            scores.append(jnp.where(qpos >= kpos, sc, -1e30))
        peak = jnp.maximum(
            jnp.max(scores[0], axis=1, keepdims=True), jnp.max(scores[1], axis=1, keepdims=True)
        )
        total = jnp.zeros((qrows, 1), F32)
        value = jnp.zeros((qrows, HEAD_SIZE), F32)
        for n in range(2):
            p = jnp.exp(scores[n] - peak)
            total = total + jnp.sum(p, axis=1, keepdims=True)
            value = value + jnp.dot(
                p.astype(BF16), kv[n, :, HEAD_SIZE:], preferred_element_type=F32
            )
        attn[h, pl.ds(r, qrows), :] = (value / total).astype(BF16)
        return carry

    lax.fori_loop(0, n_heads * (rows // qrows), attend_block, 0)

    for s in range(max(2, nd - 1), nd):
        relay_o_line(s)
        relay_o_x(s)

    mirror = (1 - c) * nd + d
    o_piece(mirror, X).wait_recv()

    @pl.when(d % 2 == 0)
    def _():
        o_piece(mirror, UP).start()

    @pl.when(d % 2 == 1)
    def _():
        o_piece(mirror, DOWN).start()

    js = nd // 2

    def out_block(b):
        full = jnp.concatenate([attn[h] for h in range(n_heads)], axis=1)
        return jnp.dot(full, go[b], preferred_element_type=F32).astype(BF16)

    def s_copy(side, j):
        i = side * js + j
        return block(sent, i, sib, i, s_send.at[i], s_recv.at[i], sibling)

    def y_copy(j):
        return block(ysend, j, yrecv, j, y_send.at[j], y_recv.at[j], across)

    near = d < js

    def arrival(i):
        pair, r = i // 2, i % 2
        group = (d // 2 + pair) % js
        mine = jnp.where(r == 0, d, e)
        return jnp.where(pair == 0, mine, group * 2 + jnp.where(near, r, 1 - r))

    for phase in range(2):
        side = c if phase == 0 else 1 - c

        def columns(i, carry):
            within = arrival(i)
            if phase == 1:

                @pl.when(within != d)
                def _():
                    o_piece(side * nd + within, X).wait_recv()

            j = within % js
            slot = side * js + j
            value = out_block(side * nd + within)
            own = within // js == k

            @pl.when(jnp.logical_not(own))
            def _():
                sent[slot] = value
                s_copy(side, j).start()

            @pl.when(own)
            def _():
                kept[slot] = value
                s_copy(side, j).wait_recv()

                @pl.when(side != y)
                def _():
                    ysend[j] = (kept[slot].astype(F32) + sib[slot].astype(F32)).astype(BF16)
                    y_copy(j).start()

            return carry

        lax.fori_loop(0, nd, columns, 0)

    cols = w_out.shape[1]
    tile[...] = jnp.zeros_like(tile)
    def finish_block(n, carry):
        j = jnp.where(near, n, js - 1 - n)
        y_copy(j).wait_recv()
        place = pl.ds(pl.multiple_of(j * cols, cols), cols)
        mine = y * js + j

        def finish(i, inner):
            rr = pl.ds(pl.multiple_of(i * chunk, chunk), chunk)
            total = (
                kept[mine, rr, :].astype(F32) + sib[mine, rr, :].astype(F32)
            ) + yrecv[j, rr, :].astype(F32)
            result = total.astype(BF16)
            out[rr, place] = result
            resid = xs[t, rr, place].astype(F32) + result.astype(F32)
            resid = resid - goal[rr, place].astype(F32)
            sq = jnp.sum((resid * resid).reshape(chunk // 8, 8, cols), axis=0)
            part = sq[:, 0:128]
            for m in range(1, cols // 128):
                part = part + sq[:, m * 128 : (m + 1) * 128]
            tile[...] += part
            return inner

        lax.fori_loop(0, rows // chunk, finish, 0)
        return carry

    lax.fori_loop(0, js, finish_block, 0)

    sums_tp[0] = tile[...]
    tp_copies = [
        block(sums_tp, 0, sums_tp, 1 + i, t_send.at[i], t_recv.at[i], where)
        for i, where in enumerate((sibling, across, diagonal))
    ]
    for copy in tp_copies:
        copy.start()
    for copy in tp_copies:
        copy.wait_recv()
    sums_all[me] = (sums_tp[0] + sums_tp[1]) + (sums_tp[2] + sums_tp[3])

    def l_copy(s, slot):
        p = (me + s) % nb
        return remote(
            sums_all.at[slot], sums_all.at[slot], l_send.at[s], l_recv.at[slot],
            {"ctx": p // nd, "dp": p % nd},
        )

    for s in range(1, nb):
        l_copy(s, me).start()
    for s in range(1, nb):
        l_copy(s, (me + s) % nb).wait_recv()
    whole = sums_all[0]
    for b in range(1, nb):
        whole = whole + sums_all[b]
    count = tp * wide * rows * nb
    loss[0, 0] = jnp.sum(whole) / count

    h_across.wait_send()
    h_sib.wait_send()
    h_relay.wait_send()
    kv_copy.wait_send()
    for copy in tp_copies:
        copy.wait_send()
    for s in range(1, nb):
        l_copy(s, me).wait_send()
    for side in range(2):
        for j in range(js):
            s_copy(side, j).wait_send()
    for j in range(js):
        y_copy(j).wait_send()
    a_piece(me, X).wait_send()
    o_piece(me, X).wait_send()
    for s in range(0, nd):
        for sign in (-1, 1) if s else (1,):
            b = me + sign * s
            there = (d + sign * s >= 0) & (d + sign * s < nd)
            if s:

                @pl.when(there)
                def _():
                    a_piece(b, X).wait_send()

                @pl.when(there & (d + sign * s != e))
                def _():
                    o_piece(b, X).wait_send()

            if s == 0 or sign < 0:

                @pl.when(there & up)
                def _():
                    a_piece(b, UP).wait_send()
                    o_piece(b, UP).wait_send()

            if s == 0 or sign > 0:

                @pl.when(there & down)
                def _():
                    a_piece(b, DOWN).wait_send()
                    o_piece(b, DOWN).wait_send()

    @pl.when(d % 2 == 0)
    def _():
        o_piece(mirror, UP).wait_send()

    @pl.when(d % 2 == 1)
    def _():
        o_piece(mirror, DOWN).wait_send()


def fused(nd, hidden, target, gain, w_query, w_key, value_matrix, w_out, block_order):
    rows, wide = hidden.shape[1:]
    nb = 2 * nd
    tp = lax.axis_size("tp")
    deep, qcols = w_query.shape
    all_cols = qcols + w_key.shape[1] + value_matrix.shape[1]
    orows, ocols = w_out.shape
    half = HEAD_SIZE // 2
    freqs = rope_base ** (-(jnp.arange(half, dtype=F32) * 2.0) / HEAD_SIZE)
    freqs = jnp.concatenate([freqs, freqs])[None, :]
    heads = qcols // HEAD_SIZE
    js = nd // 2
    vmem = pl.BlockSpec(memory_space=pltpu.VMEM)
    anyspace = pl.BlockSpec(memory_space=pl.ANY)
    dma = pltpu.SemaphoreType.DMA
    branch, loss = pl.pallas_call(
        functools.partial(layer, nd),
        out_shape=(
            jax.ShapeDtypeStruct((rows, wide), BF16),
            jax.ShapeDtypeStruct((1, 1), F32),
        ),
        in_specs=[
            pl.BlockSpec(memory_space=pltpu.SMEM),
            anyspace,
            anyspace,
            vmem,
            vmem,
            anyspace,
            anyspace,
            anyspace,
            anyspace,
        ],
        out_specs=(vmem, pl.BlockSpec(memory_space=pltpu.SMEM)),
        scratch_shapes=[
            pltpu.VMEM((nb, deep, all_cols), BF16),
            pltpu.VMEM((nb, orows, ocols), BF16),
            pltpu.VMEM((tp, rows, wide), BF16),
            pltpu.VMEM((rows, wide), BF16),
            pltpu.VMEM((nb, rows, deep), BF16),
            pltpu.VMEM((rows, all_cols), F32),
            pltpu.VMEM((2, rows, HEAD_SIZE), F32),
            pltpu.VMEM((heads, rows, HEAD_SIZE), BF16),
            pltpu.VMEM((2, rows, 2 * HEAD_SIZE), BF16),
            pltpu.VMEM((heads, rows, HEAD_SIZE), BF16),
            pltpu.VMEM((2 * js, rows, ocols), BF16),
            pltpu.VMEM((2 * js, rows, ocols), BF16),
            pltpu.VMEM((2 * js, rows, ocols), BF16),
            pltpu.VMEM((js, rows, ocols), BF16),
            pltpu.VMEM((js, rows, ocols), BF16),
            pltpu.VMEM((8, 128), F32),
            pltpu.VMEM((tp, 8, 128), F32),
            pltpu.VMEM((nb, 8, 128), F32),
            dma((6,)),
            dma((3, nb)),
            dma((nb,)),
            dma((3, nb)),
            dma((nb,)),
            dma((3,)),
            dma((3,)),
            dma((1,)),
            dma((1,)),
            dma((2 * js,)),
            dma((2 * js,)),
            dma((js,)),
            dma((js,)),
            dma((3,)),
            dma((3,)),
            dma((nb,)),
            dma((nb,)),
        ],
        compiler_params=pltpu.CompilerParams(
            collective_id=1, has_side_effects=True, vmem_limit_bytes=60 * 1024 * 1024
        ),
    )(
        block_order,
        hidden[0],
        target[0],
        gain[None, :],
        freqs,
        w_query,
        w_key,
        value_matrix,
        w_out,
    )
    return (branch[None], loss.reshape(()))


def solution(mesh):
    in_specs = (
        P("dp", "ctx", "tp"),
        P("dp", "ctx", "tp"),
        P(),
        P(("ctx", "dp"), "tp"),
        P(("ctx", "dp"), "tp"),
        P(("ctx", "dp"), "tp"),
        P("tp", ("ctx", "dp")),
        P(),
    )
    out_specs = (P("dp", "ctx", "tp"), P())
    sizes = mesh.shape
    fits = sizes["ctx"] == 2 and sizes["tp"] == 4 and sizes["dp"] % 2 == 0
    body = functools.partial(fused, sizes["dp"]) if fits else on_device
    return jax.shard_map(
        body, mesh=mesh, in_specs=in_specs, out_specs=out_specs, check_vma=False
    )
```

profile of v0, /device:TPU:0, one launch (start us, length us, event | category | flops | bytes accessed | tf_op | source)
XLA Modules:
  0.0 145.7 jit_solution(16058681304099059124)
XLA Ops:
  0.6 0.6 maximum_bitcast_fusion.freqs
  1.2 140.5 %shard_map.95 = (bf16[512,1024]{1,0:T(8,128)(2,1)}, f32[1,1]{1,0:T(1,128)}) custom-call(s32[4]{0:T(128)} %order.1, bf16[512,1024]{1,0:T(8,128)(2,1)} %bitcast.7, bf16[512,1024]{1,0:T(8,128)(2,1)} %bitcast.8, f32[1,4096]{1,0:T(1,128)} %bitcast.10, f32[1,128]{1,0:T(1,128)} %maximum_bitcast_fusion.freqs, bf16[512,512]{1,0:T(8,128)(2,1)} %w_query.1, ...), custom_call_target="tpu_custom_call" | custom-call | tf_op jit(solution)/shard_map/pallas_call | solution.py:641
  141.8 2.3 %copy.12 = bf16[1,512,1024]{2,1,0:T(8,128)(2,1)} copy(bf16[1,512,1024]{2,1,0:T(8,128)(2,1)} %bitcast.9) | data formatting | bytes 2097152
  (1 shorter events, 0.0 us)
where the time goes:
time: 146 us
  Pallas kernels  141 us (97%)
  between operations  2.33 us (2%)
  local copies, waits for them, and re-layouts  2.26 us (2%)
    pallas_call x1, Pallas kernels, fused(): pl.pallas_call(functools.partial(layer, nd), out_shape=(jax.ShapeDtypeStr...  141 us

commit v1 on v0

v1 whole, which is shorter than its diff:
```python
import functools

import jax
import jax.numpy as jnp
from jax import lax
from jax.experimental import pallas as pl
from jax.experimental.pallas import tpu as pltpu
from jax.sharding import PartitionSpec as P

MODEL_WIDTH = 4096
QUERY_HEADS = 16
KEY_VALUE_HEADS = 4
HEAD_SIZE = 128


rope_base = 500000.0


def shifted(value, axis, by):
    peers = lax.axis_size(axis)
    return lax.ppermute(value, axis, [(i, (i + by) % peers) for i in range(peers)])


def positions(order, start, rows, half):
    index = start + lax.iota(jnp.int32, rows)
    block = index // half
    slots = lax.iota(jnp.int32, order.shape[0])
    chosen = jnp.sum(jnp.where(block[:, None] == slots[None, :], order[None, :], 0), axis=1)
    return chosen * half + index % half


def apply_rotary(values, token_places):
    half = values.shape[-1] // 2
    freqs = rope_base ** (-(jnp.arange(half, dtype=jnp.float32) * 2.0) / values.shape[-1])
    angles = token_places.astype(jnp.float32)[:, None] * freqs[None, :]
    cosine = jnp.cos(angles)[:, None, :]
    sine = jnp.sin(angles)[:, None, :]
    first = values[..., :half]
    second = values[..., half:]
    return jnp.concatenate(
        [first * cosine - second * sine, second * cosine + first * sine], axis=-1
    )


def attend(state, query_rows, qpos, piece, kpos):
    peak, total, accum = state
    rows = piece.shape[1]
    local_heads = query_rows.shape[1]
    pair = piece.reshape(2, rows, local_heads, HEAD_SIZE)
    scores = jnp.einsum(
        "qcgd,kcd->cgqk", query_rows, pair[0], preferred_element_type=jnp.float32
    ) * (1.0 / HEAD_SIZE**0.5)
    allowed = (qpos[:, None] >= kpos[None, :])[None, None]
    scores = jnp.where(allowed, scores, -1e30)
    new_peak = jnp.maximum(peak, jnp.max(scores, axis=-1))
    weights = jnp.where(allowed, jnp.exp(scores - new_peak[..., None]), 0.0)
    factor = jnp.exp(peak - new_peak)
    total = total * factor + jnp.sum(weights, axis=-1)
    update = jnp.einsum(
        "cgqk,kcd->qcgd", weights.astype(jnp.bfloat16), pair[1], preferred_element_type=jnp.float32
    )
    accum = accum * jnp.transpose(factor, (2, 0, 1))[..., None] + update
    return (new_peak, total, accum)


def on_device(hidden, target, gain, w_query, w_key, value_matrix, w_out, block_order):
    rows = hidden.shape[1]
    half = rows // 2
    local = hidden[0]
    whole = lax.all_gather(local, "tp", axis=1, tiled=True)
    wide = whole.astype(jnp.float32)
    normed = (
        wide * lax.rsqrt(jnp.mean(wide * wide, axis=1, keepdims=True) + 1e-05) * gain[None, :]
    ).astype(jnp.bfloat16)
    pieces = (
        lax.all_gather(w_query, ("ctx", "dp"), axis=0, tiled=True),
        lax.all_gather(w_key, ("ctx", "dp"), axis=0, tiled=True),
        lax.all_gather(value_matrix, ("ctx", "dp"), axis=0, tiled=True),
    )
    query_rows, key, value_rows = tuple(
        (jnp.dot(normed, piece, preferred_element_type=jnp.float32) for piece in pieces)
    )
    shard = lax.axis_index("ctx")
    qpos = positions(block_order, shard * rows, rows, half)
    local_heads = w_key.shape[1] // HEAD_SIZE
    query_group = QUERY_HEADS // KEY_VALUE_HEADS
    query_rows = (
        apply_rotary(query_rows.reshape(rows, local_heads * query_group, HEAD_SIZE), qpos)
        .astype(jnp.bfloat16)
        .reshape(rows, local_heads, query_group, HEAD_SIZE)
    )
    key = (
        apply_rotary(key.reshape(rows, local_heads, HEAD_SIZE), qpos)
        .astype(jnp.bfloat16)
        .reshape(rows, local_heads * HEAD_SIZE)
    )
    pair = jnp.stack([key, value_rows.astype(jnp.bfloat16)])
    state = (
        jnp.full((local_heads, query_group, rows), -1e30, jnp.float32),
        jnp.zeros((local_heads, query_group, rows), jnp.float32),
        jnp.zeros((rows, local_heads, query_group, HEAD_SIZE), jnp.float32),
    )
    count = lax.axis_size("ctx")
    state = attend(state, query_rows, qpos, pair, qpos)

    def turn(step, carry):
        moved, inner = carry
        moved = shifted(moved, "ctx", 1)
        source = (shard - step) % count
        return (
            moved,
            attend(
                inner, query_rows, qpos, moved, positions(block_order, source * rows, rows, half)
            ),
        )

    moved_end, state = lax.fori_loop(1, count, turn, (pair, state))
    peak, total, accum = state
    attn = (
        (accum / jnp.transpose(total, (2, 0, 1))[..., None])
        .astype(jnp.bfloat16)
        .reshape(rows, local_heads * query_group * HEAD_SIZE)
    )
    terms = jnp.dot(
        attn,
        lax.all_gather(w_out, ("ctx", "dp"), axis=1, tiled=True),
        preferred_element_type=jnp.float32,
    )
    summed = lax.psum_scatter(terms.astype(jnp.bfloat16), "tp", scatter_dimension=1, tiled=True)
    resid = local.astype(jnp.float32) + summed.astype(jnp.float32) - target[0].astype(jnp.float32)
    squares = lax.psum(jnp.sum(resid * resid), ("ctx", "tp", "dp"))
    loss = squares / (lax.axis_size("dp") * lax.axis_size("ctx") * rows * MODEL_WIDTH)
    return (summed[None], loss)


MESH = pl.DeviceIdType.MESH
F32 = jnp.float32
BF16 = jnp.bfloat16


def layer(
    nd,
    order,
    hidden,
    target,
    gain,
    freqs,
    w_query,
    w_key,
    value_matrix,
    w_out,
    out,
    loss,
    ga,
    stage,
    go,
    ostage,
    mine,
    xs,
    goal,
    normed,
    acc,
    trig,
    query,
    kv,
    attn,
    made,
    arrived,
    tile,
    sums_plane,
    sums_line,
    load_sem,
    x_send,
    a_send,
    a_recv,
    oy_send,
    oy_recv,
    o_send,
    o_recv,
    h_send,
    h_recv,
    kv_send,
    kv_recv,
    at_send,
    at_recv,
    r_send,
    r_recv,
    p_send,
    p_recv,
    l_send,
    l_recv,
):
    c, t, d = lax.axis_index("ctx"), lax.axis_index("tp"), lax.axis_index("dp")
    y, k = t // 2, t % 2
    sibling = y * 2 + (1 - k)
    across = (1 - y) * 2 + k
    rows, wide = hidden.shape
    deep, qcols = w_query.shape
    half = rows // 2
    n_heads = qcols // HEAD_SIZE
    tp = 4
    plane = 2 * tp
    owner = c == k
    up, down = d < nd - 1, d > 0

    def load(i, src, dst):
        return pltpu.make_async_copy(src, dst, load_sem.at[i])

    def weight_loads(dst):
        return (
            load(0, w_query, dst.at[:, pl.ds(0, qcols)]),
            load(1, w_key, dst.at[:, pl.ds(qcols, HEAD_SIZE)]),
            load(2, value_matrix, dst.at[:, pl.ds(qcols + HEAD_SIZE, HEAD_SIZE)]),
        )

    hc = w_out.shape[1] // 2
    own_loads = weight_loads(ga.at[k * nd + d])
    stage_loads = weight_loads(stage)
    mine_load = load(3, hidden, mine)
    keep_load = load(4, w_out.at[:, pl.ds(pl.multiple_of(y * hc, hc), hc)], go.at[d, k, y])
    give_load = load(5, w_out.at[:, pl.ds(pl.multiple_of((1 - y) * hc, hc), hc)], ostage)
    local_load = load(6, hidden, xs.at[t])
    goal_load = load(7, target, goal)

    @pl.when(owner)
    def _():
        for copy in own_loads:
            copy.start()

    @pl.when(jnp.logical_not(owner))
    def _():
        for copy in stage_loads:
            copy.start()

    mine_load.start()
    give_load.start()
    keep_load.start()

    @pl.when(owner)
    def _():
        local_load.start()

    goal_load.start()

    barrier = pltpu.get_barrier_semaphore()
    seat = c * tp + t
    for s in range(1, plane):
        p = (seat + s) % plane
        pl.semaphore_signal(
            barrier, inc=1, device_id={"ctx": p // tp, "tp": p % tp}, device_id_type=MESH
        )
    for s in range(1, nd):
        pl.semaphore_signal(barrier, inc=1, device_id={"dp": (d + s) % nd}, device_id_type=MESH)
    pl.semaphore_wait(barrier, plane - 1 + nd - 1)

    def remote(src, dst, ssem, rsem, where):
        return pltpu.make_async_remote_copy(
            src_ref=src, dst_ref=dst, send_sem=ssem, recv_sem=rsem,
            device_id=where, device_id_type=MESH,
        )

    UP, DOWN, SIB = 0, 1, 2

    def target_of(way):
        return {
            UP: {"dp": jnp.minimum(d + 1, nd - 1)},
            DOWN: {"dp": jnp.maximum(d - 1, 0)},
            SIB: {"tp": sibling},
        }[way]

    def a_copy(i, way, lane=k):
        ref = ga.at[lane * nd + i]
        return remote(ref, ref, a_send.at[way, i], a_recv.at[lane * nd + i], target_of(way))

    def o_copy(i, way, lane=k):
        ref = go.at[i, lane]
        return remote(ref, ref, o_send.at[way, i], o_recv.at[lane * nd + i], target_of(way))

    def spread(copy, i, ways):
        copy_up = lambda: copy(i, UP).start()
        copy_down = lambda: copy(i, DOWN).start()
        if UP in ways:
            pl.when(up)(copy_up)
        if DOWN in ways:
            pl.when(down)(copy_down)
        copy(i, SIB).start()

    def relay(copy, s):
        @pl.when(d >= s)
        def _():
            copy(d - s, UP).wait_recv()
            spread(copy, d - s, (UP,))

        @pl.when(d + s < nd)
        def _():
            copy(d + s, DOWN).wait_recv()
            spread(copy, d + s, (DOWN,))

    x_slot = ga.at[c * nd + d]
    x_copy = remote(
        stage, x_slot, x_send.at[0], a_recv.at[c * nd + d], {"ctx": k, "tp": y * 2 + c}
    )

    @pl.when(owner)
    def _():
        for copy in own_loads:
            copy.wait()
        spread(a_copy, d, (UP, DOWN))

    @pl.when(jnp.logical_not(owner))
    def _():
        for copy in stage_loads:
            copy.wait()
        x_copy.start()

    mine_load.wait()
    h_y = remote(mine, xs.at[t], h_send.at[0], h_recv.at[t], {"tp": (1 - y) * 2 + c})
    h_x = remote(mine, xs.at[t], h_send.at[1], h_recv.at[t], {"ctx": 1 - c, "tp": y * 2 + c})
    h_sib = remote(mine, xs.at[t], h_send.at[2], h_recv.at[t], {"tp": sibling})
    h_y.start()
    h_x.start()

    @pl.when(jnp.logical_not(owner))
    def _():
        h_sib.start()

    give_load.wait()
    oy_copy = remote(ostage, go.at[d, k, y], oy_send.at[0], oy_recv.at[0], {"tp": across})
    oy_copy.start()

    def positions_of(shard, index):
        low = order[2 * shard] * half
        high = order[2 * shard + 1] * half
        return jnp.where(index < half, low + index, high + index - half)

    place = positions_of(k, lax.broadcasted_iota(jnp.int32, (rows, HEAD_SIZE), 0)).astype(F32)
    angle = place * freqs[...]
    lane_of = lax.broadcasted_iota(jnp.int32, (rows, HEAD_SIZE), 1)
    trig[0] = jnp.cos(angle)
    sine = jnp.sin(angle)
    trig[1] = jnp.where(lane_of < HEAD_SIZE // 2, -sine, sine)

    @pl.when(jnp.logical_not(owner))
    def _():
        a_copy(d, UP).wait_recv()
        spread(a_copy, d, (UP, DOWN))

    for s in range(1, min(2, nd - 1)):
        relay(a_copy, s)

    def h_wait(slot):
        remote(mine, xs.at[slot], h_send.at[0], h_recv.at[slot], {"tp": across}).wait_recv()

    far = (1 - y) * 2
    h_relay_x = remote(
        xs.at[far + 1], xs.at[far + 1], h_send.at[3], h_recv.at[far + 1], {"ctx": 1 - c}
    )
    h_relay_y = remote(
        xs.at[y * 2], xs.at[y * 2], h_send.at[3], h_recv.at[y * 2], {"tp": across}
    )

    @pl.when(owner)
    def _():
        h_wait(far + 1)
        h_relay_x.start()

    @pl.when(jnp.logical_not(owner))
    def _():
        h_wait(y * 2)
        h_relay_y.start()

    for s in range(2, nd - 1):
        relay(a_copy, s)

    keep_load.wait()
    remote(
        ostage, go.at[d, k, 1 - y], oy_send.at[0], oy_recv.at[0], {"tp": across}
    ).wait_recv()
    spread(o_copy, d, (UP, DOWN))

    @pl.when(owner)
    def _():
        local_load.wait()
        h_wait(sibling)
        h_wait(far)

    @pl.when(jnp.logical_not(owner))
    def _():
        h_wait(y * 2 + 1)
        h_wait(far)
        h_wait(far + 1)

    chunk = min(64, rows)
    per = wide // deep

    def norm_rows(i, carry):
        r = pl.multiple_of(i * chunk, chunk)
        total = jnp.zeros((chunk, 1), F32)
        for j in range(tp):
            v = xs[j, pl.ds(r, chunk), :].astype(F32)
            total = total + jnp.sum(v * v, axis=1, keepdims=True)
        scale = lax.rsqrt(total * (1.0 / (tp * wide)) + 1e-05)
        for j in range(tp):
            for m in range(per):
                v = xs[j, pl.ds(r, chunk), m * deep : (m + 1) * deep].astype(F32)
                g = gain[:, j * wide + m * deep : j * wide + (m + 1) * deep]
                normed[j * per + m, pl.ds(r, chunk), :] = (v * scale * g).astype(BF16)
        return carry

    lax.fori_loop(0, rows // chunk, norm_rows, 0)
    acc[...] = jnp.zeros_like(acc)

    def nearest(i):
        return jnp.where(d < nd // 2, i, nd - 1 - i)

    def project(i):
        b = k * nd + i
        acc[...] += jnp.dot(normed[b], ga[b], preferred_element_type=F32)
        a_copy(i, SIB, 1 - k).wait_recv()
        b = (1 - k) * nd + i
        acc[...] += jnp.dot(normed[b], ga[b], preferred_element_type=F32)

    def project_step(i, carry):
        @pl.when(i == nd - 1)
        def _():
            relay(a_copy, nd - 1)

        project(nearest(i))
        return carry

    lax.fori_loop(0, nd, project_step, 0)

    def rotated(v):
        return (v * trig[0] + pltpu.roll(v, HEAD_SIZE // 2, 1) * trig[1]).astype(BF16)

    kv[k, :, 0:HEAD_SIZE] = rotated(acc[:, qcols : qcols + HEAD_SIZE])
    kv[k, :, HEAD_SIZE:] = acc[:, qcols + HEAD_SIZE :].astype(BF16)
    kv_copy = remote(kv.at[k], kv.at[k], kv_send.at[0], kv_recv.at[0], {"tp": sibling})
    kv_copy.start()
    for h in range(n_heads):
        part = slice(h * HEAD_SIZE, (h + 1) * HEAD_SIZE)
        query[h] = rotated(acc[:, part])
    for s in range(1, min(2, nd - 1)):
        relay(o_copy, s)

    remote(kv.at[1 - k], kv.at[1 - k], kv_send.at[0], kv_recv.at[0], {"tp": sibling}).wait_recv()
    qrows = min(256, rows)
    dims = (((1,), (1,)), ((), ()))
    group = y * 2 + c
    spots = ({"ctx": 1 - c}, {"tp": across}, {"ctx": 1 - c, "tp": across})

    def at_copy(h, way):
        ref = attn.at[group * n_heads + h]
        return remote(
            ref, ref, at_send.at[way, h], at_recv.at[group * n_heads + h], spots[way]
        )

    def attend_head(h, carry):
        def attend_block(i, inner):
            r = pl.multiple_of(i * qrows, qrows)
            q = query[h, pl.ds(r, qrows), :]
            qpos = positions_of(k, r + lax.broadcasted_iota(jnp.int32, (qrows, rows), 0))
            scores = []
            for n in range(2):
                kpos = positions_of(n, lax.broadcasted_iota(jnp.int32, (qrows, rows), 1))
                sc = lax.dot_general(
                    q, kv[n, :, 0:HEAD_SIZE], dims, preferred_element_type=F32
                ) * (1.0 / HEAD_SIZE**0.5)
                scores.append(jnp.where(qpos >= kpos, sc, -1e30))
            peak = jnp.maximum(
                jnp.max(scores[0], axis=1, keepdims=True),
                jnp.max(scores[1], axis=1, keepdims=True),
            )
            total = jnp.zeros((qrows, 1), F32)
            value = jnp.zeros((qrows, HEAD_SIZE), F32)
            for n in range(2):
                p = jnp.exp(scores[n] - peak)
                total = total + jnp.sum(p, axis=1, keepdims=True)
                value = value + jnp.dot(
                    p.astype(BF16), kv[n, :, HEAD_SIZE:], preferred_element_type=F32
                )
            attn[group * n_heads + h, pl.ds(r, qrows), :] = (value / total).astype(BF16)
            return inner

        lax.fori_loop(0, rows // qrows, attend_block, 0)
        for way in (2, 0, 1):
            at_copy(h, way).start()
        return carry

    lax.fori_loop(0, n_heads, attend_head, 0)

    for s in range(2, nd - 1):
        relay(o_copy, s)

    def at_wait(i, carry):
        g = (group + 1 + i // n_heads) % tp
        ref = attn.at[g * n_heads + i % n_heads]
        remote(
            ref, ref, at_send.at[0, 0], at_recv.at[g * n_heads + i % n_heads], spots[0]
        ).wait_recv()
        return carry

    lax.fori_loop(0, (tp - 1) * n_heads, at_wait, 0)

    js = nd // 2
    orow = min(256, rows)

    def made_copy(i):
        slot = (i % js) * 2 + y
        where = {"ctx": k, "tp": c * 2 + i // js}
        return remote(made.at[i], arrived.at[slot], r_send.at[i], r_recv.at[slot], where)

    def stays(i):
        return (k == c) & (y == c) & (i // js == k)

    def out_step(n, carry):
        @pl.when(n == nd - 1)
        def _():
            relay(o_copy, nd - 1)

        i = nearest(n)
        o_copy(i, SIB, 1 - k).wait_recv()

        def out_rows(m, inner):
            rr = pl.ds(pl.multiple_of(m * orow, orow), orow)
            total = jnp.zeros((orow, hc), F32)
            for g in range(tp):
                full = jnp.concatenate(
                    [attn[g * n_heads + h, rr, :] for h in range(n_heads)], axis=1
                )
                term = jnp.dot(full, go[i, g % 2, g // 2], preferred_element_type=F32)
                total = total + term.astype(BF16).astype(F32)
            made[i, rr, :] = total.astype(BF16)
            return inner

        lax.fori_loop(0, rows // orow, out_rows, 0)

        @pl.when(jnp.logical_not(stays(i)))
        def _():
            made_copy(i).start()

        @pl.when(stays(i))
        def _():
            arrived[(i % js) * 2 + y] = made[i]

        return carry

    lax.fori_loop(0, nd, out_step, 0)
    goal_load.wait()
    tile[...] = jnp.zeros_like(tile)

    def finish_block(n, carry):
        j = jnp.where(d < nd // 2, n // 2, js - 1 - n // 2)
        side = n % 2
        slot = j * 2 + side

        @pl.when(jnp.logical_not((y == c) & (side == y) & (c == k)))
        def _():
            remote(
                made.at[0], arrived.at[slot], r_send.at[0], r_recv.at[slot], {"tp": sibling}
            ).wait_recv()

        place = pl.ds(pl.multiple_of(slot * hc, hc), hc)

        def finish(i, inner):
            rr = pl.ds(pl.multiple_of(i * chunk, chunk), chunk)
            result = arrived[slot, rr, :]
            out[rr, place] = result
            resid = mine[rr, place].astype(F32) + result.astype(F32)
            resid = resid - goal[rr, place].astype(F32)
            sq = jnp.sum((resid * resid).reshape(chunk // 8, 8, hc), axis=0)
            part = sq[:, 0:128]
            for m in range(1, hc // 128):
                part = part + sq[:, m * 128 : (m + 1) * 128]
            tile[...] += part
            return inner

        lax.fori_loop(0, rows // chunk, finish, 0)
        return carry

    lax.fori_loop(0, 2 * js, finish_block, 0)

    def p_copy(s, slot):
        p = (seat + s) % plane
        return remote(
            sums_plane.at[slot], sums_plane.at[slot], p_send.at[s], p_recv.at[slot],
            {"ctx": p // tp, "tp": p % tp},
        )

    sums_plane[seat] = tile[...]
    for s in range(1, plane):
        p_copy(s, seat).start()
    for s in range(1, plane):
        p_copy(s, (seat + s) % plane).wait_recv()
    whole = sums_plane[0]
    for b in range(1, plane):
        whole = whole + sums_plane[b]
    sums_line[d] = whole

    def l_copy(s, slot):
        return remote(
            sums_line.at[slot], sums_line.at[slot], l_send.at[s], l_recv.at[slot],
            {"dp": (d + s) % nd},
        )

    for s in range(1, nd):
        l_copy(s, d).start()
    for s in range(1, nd):
        l_copy(s, (d + s) % nd).wait_recv()
    whole = sums_line[0]
    for b in range(1, nd):
        whole = whole + sums_line[b]
    count = plane * nd * rows * wide
    loss[0, 0] = jnp.sum(whole) / count

    @pl.when(jnp.logical_not(owner))
    def _():
        x_copy.wait_send()
        h_sib.wait_send()

    h_y.wait_send()
    h_x.wait_send()
    h_relay_x.wait_send()
    oy_copy.wait_send()
    kv_copy.wait_send()

    def drain_heads(h, carry):
        for way in range(3):
            at_copy(h, way).wait_send()
        return carry

    lax.fori_loop(0, n_heads, drain_heads, 0)

    def drain_line(i, carry):
        a_copy(i, SIB).wait_send()
        o_copy(i, SIB).wait_send()

        @pl.when(up & (i <= d))
        def _():
            a_copy(i, UP).wait_send()
            o_copy(i, UP).wait_send()

        @pl.when(down & (i >= d))
        def _():
            a_copy(i, DOWN).wait_send()
            o_copy(i, DOWN).wait_send()

        @pl.when(jnp.logical_not(stays(i)))
        def _():
            made_copy(i).wait_send()

        return carry

    lax.fori_loop(0, nd, drain_line, 0)
    for s in range(1, plane):
        p_copy(s, seat).wait_send()
    for s in range(1, nd):
        l_copy(s, d).wait_send()


def fused(nd, hidden, target, gain, w_query, w_key, value_matrix, w_out, block_order):
    rows, wide = hidden.shape[1:]
    nb = 2 * nd
    tp = 4
    plane = 2 * tp
    deep, qcols = w_query.shape
    all_cols = qcols + w_key.shape[1] + value_matrix.shape[1]
    orows, ocols = w_out.shape
    hc = ocols // 2
    half = HEAD_SIZE // 2
    freqs = rope_base ** (-(jnp.arange(half, dtype=F32) * 2.0) / HEAD_SIZE)
    freqs = jnp.concatenate([freqs, freqs])[None, :]
    heads = qcols // HEAD_SIZE
    js = nd // 2
    vmem = pl.BlockSpec(memory_space=pltpu.VMEM)
    anyspace = pl.BlockSpec(memory_space=pl.ANY)
    dma = pltpu.SemaphoreType.DMA
    branch, loss = pl.pallas_call(
        functools.partial(layer, nd),
        out_shape=(
            jax.ShapeDtypeStruct((rows, wide), BF16),
            jax.ShapeDtypeStruct((1, 1), F32),
        ),
        in_specs=[
            pl.BlockSpec(memory_space=pltpu.SMEM),
            anyspace,
            anyspace,
            vmem,
            vmem,
            anyspace,
            anyspace,
            anyspace,
            anyspace,
        ],
        out_specs=(vmem, pl.BlockSpec(memory_space=pltpu.SMEM)),
        scratch_shapes=[
            pltpu.VMEM((nb, deep, all_cols), BF16),
            pltpu.VMEM((deep, all_cols), BF16),
            pltpu.VMEM((nd, 2, 2, orows, hc), BF16),
            pltpu.VMEM((orows, hc), BF16),
            pltpu.VMEM((rows, wide), BF16),
            pltpu.VMEM((tp, rows, wide), BF16),
            pltpu.VMEM((rows, wide), BF16),
            pltpu.VMEM((nb, rows, deep), BF16),
            pltpu.VMEM((rows, all_cols), F32),
            pltpu.VMEM((2, rows, HEAD_SIZE), F32),
            pltpu.VMEM((heads, rows, HEAD_SIZE), BF16),
            pltpu.VMEM((2, rows, 2 * HEAD_SIZE), BF16),
            pltpu.VMEM((tp * heads, rows, HEAD_SIZE), BF16),
            pltpu.VMEM((nd, rows, hc), BF16),
            pltpu.VMEM((2 * js, rows, hc), BF16),
            pltpu.VMEM((8, 128), F32),
            pltpu.VMEM((plane, 8, 128), F32),
            pltpu.VMEM((nd, 8, 128), F32),
            dma((8,)),
            dma((1,)),
            dma((3, nd)),
            dma((nb,)),
            dma((1,)),
            dma((1,)),
            dma((3, nd)),
            dma((nb,)),
            dma((4,)),
            dma((tp,)),
            dma((1,)),
            dma((1,)),
            dma((3, heads)),
            dma((tp * heads,)),
            dma((nd,)),
            dma((2 * js,)),
            dma((plane,)),
            dma((plane,)),
            dma((nd,)),
            dma((nd,)),
        ],
        compiler_params=pltpu.CompilerParams(
            collective_id=1, has_side_effects=True, vmem_limit_bytes=60 * 1024 * 1024
        ),
    )(
        block_order,
        hidden[0],
        target[0],
        gain[None, :],
        freqs,
        w_query,
        w_key,
        value_matrix,
        w_out,
    )
    return (branch[None], loss.reshape(()))


def solution(mesh):
    in_specs = (
        P("dp", "ctx", "tp"),
        P("dp", "ctx", "tp"),
        P(),
        P(("ctx", "dp"), "tp"),
        P(("ctx", "dp"), "tp"),
        P(("ctx", "dp"), "tp"),
        P("tp", ("ctx", "dp")),
        P(),
    )
    out_specs = (P("dp", "ctx", "tp"), P())
    sizes = mesh.shape
    fits = sizes["ctx"] == 2 and sizes["tp"] == 4 and sizes["dp"] % 2 == 0
    body = functools.partial(fused, sizes["dp"]) if fits else on_device
    return jax.shard_map(
        body, mesh=mesh, in_specs=in_specs, out_specs=out_specs, check_vma=False
    )
```

time: 146 us -> 132 us (0.904)
  Pallas kernels: 141 us -> 126 us
    pallas_call x1, Pallas kernels: 141 us -> 126 us  [fused(): pl.pallas_call(functools.partial(layer, nd), out_shape=(jax.ShapeDtypeStr...]
where the time goes in v1:
time: 132 us; the launch traced here: 131 us
  Pallas kernels  126 us (95%)
  between operations  2.33 us (2%)
  local copies, waits for them, and re-layouts  2.26 us (2%)
    pallas_call x1, Pallas kernels, fused(): pl.pallas_call(functools.partial(layer, nd), out_shape=(jax.ShapeDtypeStr...  126 us

profile of v1, /device:TPU:0, one launch (start us, length us, event | category | flops | bytes accessed | tf_op | source)
XLA Modules:
  0.0 131.4 jit_solution(15457540476103825142)
XLA Ops:
  0.6 0.6 maximum_bitcast_fusion.freqs
  1.2 126.2 %shard_map.95 = (bf16[512,1024]{1,0:T(8,128)(2,1)}, f32[1,1]{1,0:T(1,128)}) custom-call(s32[4]{0:T(128)} %order.1, bf16[512,1024]{1,0:T(8,128)(2,1)} %bitcast.7, bf16[512,1024]{1,0:T(8,128)(2,1)} %bitcast.8, f32[1,4096]{1,0:T(1,128)} %bitcast.10, f32[1,128]{1,0:T(1,128)} %maximum_bitcast_fusion.freqs, bf16[512,512]{1,0:T(8,128)(2,1)} %w_query.1, ...), custom_call_target="tpu_custom_call" | custom-call | tf_op jit(solution)/shard_map/pallas_call | solution.py:678
  127.4 2.3 %copy.12 = bf16[1,512,1024]{2,1,0:T(8,128)(2,1)} copy(bf16[1,512,1024]{2,1,0:T(8,128)(2,1)} %bitcast.9) | data formatting | bytes 2097152
  (1 shorter events, 0.0 us)

commit v2 on v1

--- a/solution.py
+++ b/solution.py
@@ -1,6 +1,7 @@
 import functools
 
 import jax
+import numpy as np
 import jax.numpy as jnp
 from jax import lax
 from jax.experimental import pallas as pl
@@ -167,9 +168,11 @@
     made,
     arrived,
     tile,
-    sums_plane,
-    sums_line,
+    sums,
+    gains,
+    turns,
     load_sem,
+    out_sem,
     x_send,
     a_send,
     a_recv,
@@ -185,8 +188,6 @@
     at_recv,
     r_send,
     r_recv,
-    p_send,
-    p_recv,
     l_send,
     l_recv,
 ):
@@ -206,21 +207,31 @@
     def load(i, src, dst):
         return pltpu.make_async_copy(src, dst, load_sem.at[i])
 
+    hd = deep // 2
+
     def weight_loads(dst):
-        return (
-            load(0, w_query, dst.at[:, pl.ds(0, qcols)]),
-            load(1, w_key, dst.at[:, pl.ds(qcols, HEAD_SIZE)]),
-            load(2, value_matrix, dst.at[:, pl.ds(qcols + HEAD_SIZE, HEAD_SIZE)]),
-        )
+        copies = []
+        for h in range(2):
+            part, first = dst.at[h], pl.ds(h * hd, hd)
+            for src, start in (
+                (w_query, 0),
+                (w_key, qcols),
+                (value_matrix, qcols + HEAD_SIZE),
+            ):
+                there = part.at[:, pl.ds(start, src.shape[1])]
+                copies.append(load(len(copies), src.at[first], there))
+        return copies
 
     hc = w_out.shape[1] // 2
-    own_loads = weight_loads(ga.at[k * nd + d])
+    own_loads = weight_loads(ga.at[c * nd + d])
     stage_loads = weight_loads(stage)
-    mine_load = load(3, hidden, mine)
-    keep_load = load(4, w_out.at[:, pl.ds(pl.multiple_of(y * hc, hc), hc)], go.at[d, k, y])
-    give_load = load(5, w_out.at[:, pl.ds(pl.multiple_of((1 - y) * hc, hc), hc)], ostage)
-    local_load = load(6, hidden, xs.at[t])
-    goal_load = load(7, target, goal)
+    mine_load = load(6, hidden, mine)
+    keep_load = load(7, w_out.at[:, pl.ds(pl.multiple_of(y * hc, hc), hc)], go.at[d, k, y])
+    give_load = load(8, w_out.at[:, pl.ds(pl.multiple_of((1 - y) * hc, hc), hc)], ostage)
+    local_load = load(9, hidden, xs.at[t])
+    goal_load = load(10, target, goal)
+    gain_load = load(11, gain, gains)
+    turn_load = load(12, freqs, turns)
 
     @pl.when(owner)
     def _():
@@ -233,6 +244,7 @@
             copy.start()
 
     mine_load.start()
+    turn_load.start()
     give_load.start()
     keep_load.start()
 
@@ -241,6 +253,7 @@
         local_load.start()
 
     goal_load.start()
+    gain_load.start()
 
     barrier = pltpu.get_barrier_semaphore()
     seat = c * tp + t
@@ -249,9 +262,13 @@
         pl.semaphore_signal(
             barrier, inc=1, device_id={"ctx": p // tp, "tp": p % tp}, device_id_type=MESH
         )
-    for s in range(1, nd):
-        pl.semaphore_signal(barrier, inc=1, device_id={"dp": (d + s) % nd}, device_id_type=MESH)
-    pl.semaphore_wait(barrier, plane - 1 + nd - 1)
+    for there, step in ((up, 1), (down, -1)):
+
+        @pl.when(there)
+        def _():
+            pl.semaphore_signal(barrier, inc=1, device_id={"dp": d + step}, device_id_type=MESH)
+
+    pl.semaphore_wait(barrier, plane - 1 + up.astype(jnp.int32) + down.astype(jnp.int32))
 
     def remote(src, dst, ssem, rsem, where):
         return pltpu.make_async_remote_copy(
@@ -268,9 +285,10 @@
             SIB: {"tp": sibling},
         }[way]
 
-    def a_copy(i, way, lane=k):
-        ref = ga.at[lane * nd + i]
-        return remote(ref, ref, a_send.at[way, i], a_recv.at[lane * nd + i], target_of(way))
+    def a_copy(line, i, way, piece=k):
+        b = line * nd + i
+        ref = ga.at[b, piece]
+        return remote(ref, ref, a_send.at[way, b], a_recv.at[b, piece], target_of(way))
 
     def o_copy(i, way, lane=k):
         ref = go.at[i, lane]
@@ -283,46 +301,70 @@
             pl.when(up)(copy_up)
         if DOWN in ways:
             pl.when(down)(copy_down)
-        copy(i, SIB).start()
+        if SIB in ways:
+            copy(i, SIB).start()
 
     def relay(copy, s):
         @pl.when(d >= s)
         def _():
             copy(d - s, UP).wait_recv()
-            spread(copy, d - s, (UP,))
+            spread(copy, d - s, (UP, SIB))
 
         @pl.when(d + s < nd)
         def _():
             copy(d + s, DOWN).wait_recv()
-            spread(copy, d + s, (DOWN,))
-
-    x_slot = ga.at[c * nd + d]
-    x_copy = remote(
-        stage, x_slot, x_send.at[0], a_recv.at[c * nd + d], {"ctx": k, "tp": y * 2 + c}
-    )
+            spread(copy, d + s, (DOWN, SIB))
+
+    near_copy = functools.partial(a_copy, c)
+    far_copy = functools.partial(a_copy, 1 - c)
+    b_own = c * nd + d
+    half_copy = remote(
+        ga.at[b_own, 1 - k],
+        ga.at[b_own, 1 - k],
+        x_send.at[2],
+        a_recv.at[b_own, 1 - k],
+        {"tp": sibling},
+    )
+    x_copies = [
+        remote(
+            stage.at[h],
+            ga.at[b_own, h],
+            x_send.at[h],
+            a_recv.at[b_own, h],
+            {"ctx": 1 - c, "tp": y * 2 + h},
+        )
+        for h in range(2)
+    ]
 
     @pl.when(owner)
     def _():
         for copy in own_loads:
             copy.wait()
-        spread(a_copy, d, (UP, DOWN))
+        half_copy.start()
+        spread(near_copy, d, (UP, DOWN, SIB))
 
     @pl.when(jnp.logical_not(owner))
     def _():
         for copy in stage_loads:
             copy.wait()
-        x_copy.start()
+        for copy in x_copies:
+            copy.start()
 
     mine_load.wait()
     h_y = remote(mine, xs.at[t], h_send.at[0], h_recv.at[t], {"tp": (1 - y) * 2 + c})
     h_x = remote(mine, xs.at[t], h_send.at[1], h_recv.at[t], {"ctx": 1 - c, "tp": y * 2 + c})
     h_sib = remote(mine, xs.at[t], h_send.at[2], h_recv.at[t], {"tp": sibling})
     h_y.start()
-    h_x.start()
+
+    @pl.when(jnp.logical_not(owner) & (k == 0))
+    def _():
+        h_x.start()
 
     @pl.when(jnp.logical_not(owner))
     def _():
         h_sib.start()
+        near_copy(d, UP).wait_recv()
+        spread(near_copy, d, (UP, DOWN))
 
     give_load.wait()
     oy_copy = remote(ostage, go.at[d, k, y], oy_send.at[0], oy_recv.at[0], {"tp": across})
@@ -333,20 +375,30 @@
         high = order[2 * shard + 1] * half
         return jnp.where(index < half, low + index, high + index - half)
 
+    turn_load.wait()
     place = positions_of(k, lax.broadcasted_iota(jnp.int32, (rows, HEAD_SIZE), 0)).astype(F32)
-    angle = place * freqs[...]
+    angle = place * turns[...]
     lane_of = lax.broadcasted_iota(jnp.int32, (rows, HEAD_SIZE), 1)
     trig[0] = jnp.cos(angle)
     sine = jnp.sin(angle)
     trig[1] = jnp.where(lane_of < HEAD_SIZE // 2, -sine, sine)
 
-    @pl.when(jnp.logical_not(owner))
-    def _():
-        a_copy(d, UP).wait_recv()
-        spread(a_copy, d, (UP, DOWN))
-
     for s in range(1, min(2, nd - 1)):
-        relay(a_copy, s)
+        relay(near_copy, s)
+
+    @pl.when(owner & (k == 0))
+    def _():
+        h_x.start()
+
+    far_copy(d, UP).wait_recv()
+    spread(far_copy, d, (UP, DOWN, SIB))
+
+    for s in range(2, nd - 1):
+        relay(near_copy, s)
+
+    @pl.when(k == 1)
+    def _():
+        h_x.start()
 
     def h_wait(slot):
         remote(mine, xs.at[slot], h_send.at[0], h_recv.at[slot], {"tp": across}).wait_recv()
@@ -369,14 +421,17 @@
         h_wait(y * 2)
         h_relay_y.start()
 
+    for s in range(1, min(2, nd - 1)):
+        relay(far_copy, s)
+
     for s in range(2, nd - 1):
-        relay(a_copy, s)
+        relay(far_copy, s)
 
     keep_load.wait()
     remote(
         ostage, go.at[d, k, 1 - y], oy_send.at[0], oy_recv.at[0], {"tp": across}
     ).wait_recv()
-    spread(o_copy, d, (UP, DOWN))
+    spread(o_copy, d, (UP, DOWN, SIB))
 
     @pl.when(owner)
     def _():
@@ -390,6 +445,7 @@
         h_wait(far)
         h_wait(far + 1)
 
+    gain_load.wait()
     chunk = min(64, rows)
     per = wide // deep
 
@@ -403,7 +459,7 @@
         for j in range(tp):
             for m in range(per):
                 v = xs[j, pl.ds(r, chunk), m * deep : (m + 1) * deep].astype(F32)
-                g = gain[:, j * wide + m * deep : j * wide + (m + 1) * deep]
+                g = gains[:, j * wide + m * deep : j * wide + (m + 1) * deep]
                 normed[j * per + m, pl.ds(r, chunk), :] = (v * scale * g).astype(BF16)
         return carry
 
@@ -413,19 +469,28 @@
     def nearest(i):
         return jnp.where(d < nd // 2, i, nd - 1 - i)
 
-    def project(i):
-        b = k * nd + i
-        acc[...] += jnp.dot(normed[b], ga[b], preferred_element_type=F32)
-        a_copy(i, SIB, 1 - k).wait_recv()
-        b = (1 - k) * nd + i
-        acc[...] += jnp.dot(normed[b], ga[b], preferred_element_type=F32)
+    def project(i, line):
+        b = line * nd + i
+
+        @pl.when(jnp.logical_not(owner & (b == b_own)))
+        def _():
+            a_copy(line, i, SIB, 1 - k).wait_recv()
+
+        weights = ga[b].reshape(deep, ga.shape[3])
+        acc[...] += jnp.dot(normed[b], weights, preferred_element_type=F32)
 
     def project_step(i, carry):
         @pl.when(i == nd - 1)
         def _():
-            relay(a_copy, nd - 1)
-
-        project(nearest(i))
+            relay(near_copy, nd - 1)
+
+        project(nearest(i), c)
+
+        @pl.when(i == nd - 1)
+        def _():
+            relay(far_copy, nd - 1)
+
+        project(nearest(i), 1 - c)
         return carry
 
     lax.fori_loop(0, nd, project_step, 0)
@@ -440,20 +505,18 @@
     for h in range(n_heads):
         part = slice(h * HEAD_SIZE, (h + 1) * HEAD_SIZE)
         query[h] = rotated(acc[:, part])
-    for s in range(1, min(2, nd - 1)):
-        relay(o_copy, s)
-
     remote(kv.at[1 - k], kv.at[1 - k], kv_send.at[0], kv_recv.at[0], {"tp": sibling}).wait_recv()
     qrows = min(256, rows)
     dims = (((1,), (1,)), ((), ()))
     group = y * 2 + c
-    spots = ({"ctx": 1 - c}, {"tp": across}, {"ctx": 1 - c, "tp": across})
-
-    def at_copy(h, way):
-        ref = attn.at[group * n_heads + h]
-        return remote(
-            ref, ref, at_send.at[way, h], at_recv.at[group * n_heads + h], spots[way]
-        )
+    spots = ({"ctx": 1 - c}, {"tp": across})
+    x_group, y_group = y * 2 + 1 - c, (1 - y) * 2 + c
+
+    def at_copy(h, way, source=group):
+        b = source * n_heads + h
+        ref = attn.at[b]
+        sem = at_send.at[way, jnp.where(source == group, 0, n_heads) + h]
+        return remote(ref, ref, sem, at_recv.at[b], spots[way])
 
     def attend_head(h, carry):
         def attend_block(i, inner):
@@ -483,24 +546,43 @@
             return inner
 
         lax.fori_loop(0, rows // qrows, attend_block, 0)
-        for way in (2, 0, 1):
+        for way in range(2):
             at_copy(h, way).start()
         return carry
 
     lax.fori_loop(0, n_heads, attend_head, 0)
+
+    for s in range(1, min(2, nd - 1)):
+        relay(o_copy, s)
+
+    early = n_heads // 2
+
+    def at_relay(h, carry):
+        at_copy(h, 0, x_group).wait_recv()
+        at_copy(h, 1, x_group).start()
+        at_copy(early + h, 1, y_group).wait_recv()
+        at_copy(early + h, 0, y_group).start()
+        return carry
+
+    lax.fori_loop(0, early, at_relay, 0)
 
     for s in range(2, nd - 1):
         relay(o_copy, s)
 
-    def at_wait(i, carry):
-        g = (group + 1 + i // n_heads) % tp
-        ref = attn.at[g * n_heads + i % n_heads]
-        remote(
-            ref, ref, at_send.at[0, 0], at_recv.at[g * n_heads + i % n_heads], spots[0]
-        ).wait_recv()
-        return carry
-
-    lax.fori_loop(0, (tp - 1) * n_heads, at_wait, 0)
+
+    def at_wait(h, carry):
+        at_copy(early + h, 0, x_group).wait_recv()
+        at_copy(h, 1, y_group).wait_recv()
+        return carry
+
+    lax.fori_loop(0, early, at_wait, 0)
+    z_group = (1 - y) * 2 + 1 - c
+
+    def far_wait(h, carry):
+        at_copy(h, 1, z_group).wait_recv()
+        return carry
+
+    lax.fori_loop(0, n_heads, far_wait, 0)
 
     js = nd // 2
     orow = min(256, rows)
@@ -549,6 +631,10 @@
     goal_load.wait()
     tile[...] = jnp.zeros_like(tile)
 
+    def out_copy(slot):
+        place = pl.ds(pl.multiple_of(slot * hc, hc), hc)
+        return pltpu.make_async_copy(arrived.at[slot], out.at[:, place], out_sem.at[slot])
+
     def finish_block(n, carry):
         j = jnp.where(d < nd // 2, n // 2, js - 1 - n // 2)
         side = n % 2
@@ -560,12 +646,12 @@
                 made.at[0], arrived.at[slot], r_send.at[0], r_recv.at[slot], {"tp": sibling}
             ).wait_recv()
 
+        out_copy(slot).start()
         place = pl.ds(pl.multiple_of(slot * hc, hc), hc)
 
         def finish(i, inner):
             rr = pl.ds(pl.multiple_of(i * chunk, chunk), chunk)
             result = arrived[slot, rr, :]
-            out[rr, place] = result
             resid = mine[rr, place].astype(F32) + result.astype(F32)
             resid = resid - goal[rr, place].astype(F32)
             sq = jnp.sum((resid * resid).reshape(chunk // 8, 8, hc), axis=0)
@@ -580,44 +666,47 @@
 
     lax.fori_loop(0, 2 * js, finish_block, 0)
 
-    def p_copy(s, slot):
-        p = (seat + s) % plane
+    everyone = plane * nd
+    number = d * plane + seat
+
+    def l_copy(s, slot):
+        p = (number + s) % everyone
         return remote(
-            sums_plane.at[slot], sums_plane.at[slot], p_send.at[s], p_recv.at[slot],
-            {"ctx": p // tp, "tp": p % tp},
+            sums.at[slot], sums.at[slot], l_send.at[s], l_recv.at[slot],
+            {"ctx": p % plane // tp, "tp": p % tp, "dp": p // plane},
         )
 
-    sums_plane[seat] = tile[...]
-    for s in range(1, plane):
-        p_copy(s, seat).start()
-    for s in range(1, plane):
-        p_copy(s, (seat + s) % plane).wait_recv()
-    whole = sums_plane[0]
-    for b in range(1, plane):
-        whole = whole + sums_plane[b]
-    sums_line[d] = whole
-
-    def l_copy(s, slot):
-        return remote(
-            sums_line.at[slot], sums_line.at[slot], l_send.at[s], l_recv.at[slot],
-            {"dp": (d + s) % nd},
-        )
-
-    for s in range(1, nd):
-        l_copy(s, d).start()
-    for s in range(1, nd):
-        l_copy(s, (d + s) % nd).wait_recv()
-    whole = sums_line[0]
-    for b in range(1, nd):
-        whole = whole + sums_line[b]
+    sums[number] = tile[...]
+
+    def share(s, carry):
+        l_copy(s, number).start()
+        return carry
+
+    lax.fori_loop(1, everyone, share, 0)
+
+    def collect(s, carry):
+        l_copy(s, (number + s) % everyone).wait_recv()
+        return carry
+
+    lax.fori_loop(1, everyone, collect, 0)
+    whole = sums[0]
+    for b in range(1, everyone):
+        whole = whole + sums[b]
     count = plane * nd * rows * wide
     loss[0, 0] = jnp.sum(whole) / count
 
+    @pl.when(owner)
+    def _():
+        half_copy.wait_send()
+
     @pl.when(jnp.logical_not(owner))
     def _():
-        x_copy.wait_send()
+        for copy in x_copies:
+            copy.wait_send()
         h_sib.wait_send()
 
+    for slot in range(2 * js):
+        out_copy(slot).wait()
     h_y.wait_send()
     h_x.wait_send()
     h_relay_x.wait_send()
@@ -625,25 +714,35 @@
     kv_copy.wait_send()
 
     def drain_heads(h, carry):
-        for way in range(3):
+        for way in range(2):
             at_copy(h, way).wait_send()
         return carry
 
     lax.fori_loop(0, n_heads, drain_heads, 0)
 
+    def drain_relays(h, carry):
+        at_copy(h, 1, x_group).wait_send()
+        at_copy(early + h, 0, y_group).wait_send()
+        return carry
+
+    lax.fori_loop(0, early, drain_relays, 0)
+
     def drain_line(i, carry):
-        a_copy(i, SIB).wait_send()
+        @pl.when(owner | (i != d))
+        def _():
+            near_copy(i, SIB).wait_send()
+
+        far_copy(i, SIB).wait_send()
         o_copy(i, SIB).wait_send()
-
-        @pl.when(up & (i <= d))
-        def _():
-            a_copy(i, UP).wait_send()
-            o_copy(i, UP).wait_send()
-
-        @pl.when(down & (i >= d))
-        def _():
-            a_copy(i, DOWN).wait_send()
-            o_copy(i, DOWN).wait_send()
+        for copy in (near_copy, far_copy, o_copy):
+
+            @pl.when(up & (i <= d))
+            def _():
+                copy(i, UP).wait_send()
+
+            @pl.when(down & (i >= d))
+            def _():
+                copy(i, DOWN).wait_send()
 
         @pl.when(jnp.logical_not(stays(i)))
         def _():
@@ -652,10 +751,11 @@
         return carry
 
     lax.fori_loop(0, nd, drain_line, 0)
-    for s in range(1, plane):
-        p_copy(s, seat).wait_send()
-    for s in range(1, nd):
-        l_copy(s, d).wait_send()
+    def drain_sums(s, carry):
+        l_copy(s, number).wait_send()
+        return carry
+
+    lax.fori_loop(1, everyone, drain_sums, 0)
 
 
 def fused(nd, hidden, target, gain, w_query, w_key, value_matrix, w_out, block_order):
@@ -668,11 +768,10 @@
     orows, ocols = w_out.shape
     hc = ocols // 2
     half = HEAD_SIZE // 2
-    freqs = rope_base ** (-(jnp.arange(half, dtype=F32) * 2.0) / HEAD_SIZE)
-    freqs = jnp.concatenate([freqs, freqs])[None, :]
+    freqs = np.float64(rope_base) ** (-np.arange(half) * 2.0 / HEAD_SIZE)
+    freqs = jnp.asarray(np.concatenate([freqs, freqs])[None, :].astype(np.float32))
     heads = qcols // HEAD_SIZE
     js = nd // 2
-    vmem = pl.BlockSpec(memory_space=pltpu.VMEM)
     anyspace = pl.BlockSpec(memory_space=pl.ANY)
     dma = pltpu.SemaphoreType.DMA
     branch, loss = pl.pallas_call(
@@ -685,17 +784,17 @@
             pl.BlockSpec(memory_space=pltpu.SMEM),
             anyspace,
             anyspace,
-            vmem,
-            vmem,
+            anyspace,
+            anyspace,
             anyspace,
             anyspace,
             anyspace,
             anyspace,
         ],
-        out_specs=(vmem, pl.BlockSpec(memory_space=pltpu.SMEM)),
+        out_specs=(anyspace, pl.BlockSpec(memory_space=pltpu.SMEM)),
         scratch_shapes=[
-            pltpu.VMEM((nb, deep, all_cols), BF16),
-            pltpu.VMEM((deep, all_cols), BF16),
+            pltpu.VMEM((nb, 2, deep // 2, all_cols), BF16),
+            pltpu.VMEM((2, deep // 2, all_cols), BF16),
             pltpu.VMEM((nd, 2, 2, orows, hc), BF16),
             pltpu.VMEM((orows, hc), BF16),
             pltpu.VMEM((rows, wide), BF16),
@@ -710,12 +809,14 @@
             pltpu.VMEM((nd, rows, hc), BF16),
             pltpu.VMEM((2 * js, rows, hc), BF16),
             pltpu.VMEM((8, 128), F32),
-            pltpu.VMEM((plane, 8, 128), F32),
-            pltpu.VMEM((nd, 8, 128), F32),
-            dma((8,)),
-            dma((1,)),
-            dma((3, nd)),
-            dma((nb,)),
+            pltpu.VMEM((plane * nd, 8, 128), F32),
+            pltpu.VMEM((1, tp * wide), F32),
+            pltpu.VMEM((1, HEAD_SIZE), F32),
+            dma((13,)),
+            dma((2 * js,)),
+            dma((3,)),
+            dma((3, nb)),
+            dma((nb, 2)),
             dma((1,)),
             dma((1,)),
             dma((3, nd)),
@@ -724,14 +825,12 @@
             dma((tp,)),
             dma((1,)),
             dma((1,)),
-            dma((3, heads)),
+            dma((2, 2 * heads)),
             dma((tp * heads,)),
             dma((nd,)),
             dma((2 * js,)),
-            dma((plane,)),
-            dma((plane,)),
-            dma((nd,)),
-            dma((nd,)),
+            dma((plane * nd,)),
+            dma((plane * nd,)),
         ],
         compiler_params=pltpu.CompilerParams(
             collective_id=1, has_side_effects=True, vmem_limit_bytes=60 * 1024 * 1024

time: 132 us -> 114 us (0.86)
  Pallas kernels: 126 us -> 109 us
    pallas_call x1, Pallas kernels: 126 us -> 109 us  [fused(): pl.pallas_call(functools.partial(layer, nd), out_shape=(jax.ShapeDtypeStr...]
where the time goes in v2:
time: 114 us; the launch traced here: 113 us
  Pallas kernels  109 us (96%)
  between operations  2.33 us (2%)
  local copies, waits for them, and re-layouts  2.26 us (2%)
    pallas_call x1, Pallas kernels, fused(): pl.pallas_call(functools.partial(layer, nd), out_shape=(jax.ShapeDtypeStr...  109 us

profile of v2, /device:TPU:0, one launch (start us, length us, event | category | flops | bytes accessed | tf_op | source)
XLA Modules:
  0.0 113.4 jit_solution(14826543719533676207)
XLA Ops:
  0.6 108.8 %shard_map.104 = (bf16[512,1024]{1,0:T(8,128)(2,1)}, f32[1,1]{1,0:T(1,128)}) custom-call(s32[4]{0:T(128)} %order.1, bf16[512,1024]{1,0:T(8,128)(2,1)} %bitcast.5, bf16[512,1024]{1,0:T(8,128)(2,1)} %bitcast.6, f32[1,4096]{1,0:T(1,128)} %bitcast.8, f32[1,128]{1,0:T(1,128)} %constant.2.clone.freqs, bf16[512,512]{1,0:T(8,128)(2,1)} %w_query.1, ...), custom_call_target="tpu_custom_call" | custom-call | tf_op jit(solution)/shard_map/pallas_call | solution.py:777
  109.4 2.3 %copy.13 = bf16[1,512,1024]{2,1,0:T(8,128)(2,1)} copy(bf16[1,512,1024]{2,1,0:T(8,128)(2,1)} %bitcast.7) | data formatting | bytes 2097152

commit v3 on v2

--- a/solution.py
+++ b/solution.py
@@ -141,7 +141,7 @@
 
 def layer(
     nd,
-    order,
+    order_in,
     hidden,
     target,
     gain,
@@ -171,8 +171,8 @@
     sums,
     gains,
     turns,
+    order,
     load_sem,
-    out_sem,
     x_send,
     a_send,
     a_recv,
@@ -207,31 +207,38 @@
     def load(i, src, dst):
         return pltpu.make_async_copy(src, dst, load_sem.at[i])
 
-    hd = deep // 2
+    quarter = deep // 4
+
+    def rows_of(piece):
+        return pl.ds(pl.multiple_of(piece * quarter, quarter), quarter)
 
     def weight_loads(dst):
-        copies = []
-        for h in range(2):
-            part, first = dst.at[h], pl.ds(h * hd, hd)
-            for src, start in (
-                (w_query, 0),
-                (w_key, qcols),
-                (value_matrix, qcols + HEAD_SIZE),
-            ):
-                there = part.at[:, pl.ds(start, src.shape[1])]
-                copies.append(load(len(copies), src.at[first], there))
-        return copies
+        return (
+            load(0, w_query, dst.at[:, pl.ds(0, qcols)]),
+            load(1, w_key, dst.at[:, pl.ds(qcols, HEAD_SIZE)]),
+            load(2, value_matrix, dst.at[:, pl.ds(qcols + HEAD_SIZE, HEAD_SIZE)]),
+        )
 
     hc = w_out.shape[1] // 2
+    hq = hc // 2
     own_loads = weight_loads(ga.at[c * nd + d])
     stage_loads = weight_loads(stage)
-    mine_load = load(6, hidden, mine)
-    keep_load = load(7, w_out.at[:, pl.ds(pl.multiple_of(y * hc, hc), hc)], go.at[d, k, y])
-    give_load = load(8, w_out.at[:, pl.ds(pl.multiple_of((1 - y) * hc, hc), hc)], ostage)
-    local_load = load(9, hidden, xs.at[t])
-    goal_load = load(10, target, goal)
-    gain_load = load(11, gain, gains)
-    turn_load = load(12, freqs, turns)
+    mine_load = load(3, hidden, mine)
+
+    def columns_of(half_of, part):
+        return pl.ds(pl.multiple_of(half_of * hc + part * hq, hq), hq)
+
+    keep_loads = [
+        load(4 + e, w_out.at[:, columns_of(y, e)], go.at[d, k, e, y]) for e in range(2)
+    ]
+    give_loads = [
+        load(6 + e, w_out.at[:, columns_of(1 - y, e)], ostage.at[e]) for e in range(2)
+    ]
+    local_load = load(8, hidden, xs.at[t])
+    goal_load = load(9, target, goal)
+    gain_load = load(10, gain, gains)
+    turn_load = load(11, freqs, turns)
+    order_load = load(12, order_in, order)
 
     @pl.when(owner)
     def _():
@@ -244,9 +251,10 @@
             copy.start()
 
     mine_load.start()
+    order_load.start()
     turn_load.start()
-    give_load.start()
-    keep_load.start()
+    for copy in give_loads + keep_loads:
+        copy.start()
 
     @pl.when(owner)
     def _():
@@ -285,63 +293,73 @@
             SIB: {"tp": sibling},
         }[way]
 
-    def a_copy(line, i, way, piece=k):
-        b = line * nd + i
-        ref = ga.at[b, piece]
-        return remote(ref, ref, a_send.at[way, b], a_recv.at[b, piece], target_of(way))
-
-    def o_copy(i, way, lane=k):
-        ref = go.at[i, lane]
-        return remote(ref, ref, o_send.at[way, i], o_recv.at[lane * nd + i], target_of(way))
-
-    def spread(copy, i, ways):
-        copy_up = lambda: copy(i, UP).start()
-        copy_down = lambda: copy(i, DOWN).start()
+    def a_copy(line, i, way, e, core=k):
+        b, piece = line * nd + i, 2 * core + e
+        ref = ga.at[b, rows_of(piece)]
+        return remote(ref, ref, a_send.at[way, b, e], a_recv.at[b, piece], target_of(way))
+
+    def o_copy(i, way, e, core=k):
+        ref = go.at[i, core, e]
+        return remote(
+            ref, ref, o_send.at[way, i, e], o_recv.at[core * nd + i, e], target_of(way)
+        )
+
+    def spread(copy, i, ways, e):
+        copy_up = lambda: copy(i, UP, e).start()
+        copy_down = lambda: copy(i, DOWN, e).start()
         if UP in ways:
             pl.when(up)(copy_up)
         if DOWN in ways:
             pl.when(down)(copy_down)
         if SIB in ways:
-            copy(i, SIB).start()
-
-    def relay(copy, s):
-        @pl.when(d >= s)
-        def _():
-            copy(d - s, UP).wait_recv()
-            spread(copy, d - s, (UP, SIB))
-
-        @pl.when(d + s < nd)
-        def _():
-            copy(d + s, DOWN).wait_recv()
-            spread(copy, d + s, (DOWN, SIB))
+            copy(i, SIB, e).start()
+
+    def relay(copy, s, parts=(0, 1)):
+        for e in parts:
+
+            @pl.when(d >= s)
+            def _():
+                copy(d - s, UP, e).wait_recv()
+                spread(copy, d - s, (UP, SIB), e)
+
+            @pl.when(d + s < nd)
+            def _():
+                copy(d + s, DOWN, e).wait_recv()
+                spread(copy, d + s, (DOWN, SIB), e)
 
     near_copy = functools.partial(a_copy, c)
     far_copy = functools.partial(a_copy, 1 - c)
     b_own = c * nd + d
-    half_copy = remote(
-        ga.at[b_own, 1 - k],
-        ga.at[b_own, 1 - k],
-        x_send.at[2],
-        a_recv.at[b_own, 1 - k],
-        {"tp": sibling},
-    )
-    x_copies = [
-        remote(
-            stage.at[h],
-            ga.at[b_own, h],
-            x_send.at[h],
-            a_recv.at[b_own, h],
-            {"ctx": 1 - c, "tp": y * 2 + h},
-        )
-        for h in range(2)
-    ]
+    half_copies = []
+    x_copies = []
+    for e in range(2):
+        ref = ga.at[b_own, rows_of(2 * (1 - k) + e)]
+        half_copies.append(
+            remote(
+                ref, ref, x_send.at[4 + e], a_recv.at[b_own, 2 * (1 - k) + e], {"tp": sibling}
+            )
+        )
+        for h in range(2):
+            piece = 2 * h + e
+            x_copies.append(
+                remote(
+                    stage.at[rows_of(piece)],
+                    ga.at[b_own, rows_of(piece)],
+                    x_send.at[piece],
+                    a_recv.at[b_own, piece],
+                    {"ctx": 1 - c, "tp": y * 2 + h},
+                )
+            )
 
     @pl.when(owner)
     def _():
         for copy in own_loads:
             copy.wait()
-        half_copy.start()
-        spread(near_copy, d, (UP, DOWN, SIB))
+        for e in range(2):
+            half_copies[e].start()
+            spread(near_copy, d, (UP, DOWN), e)
+        for e in range(2):
+            spread(near_copy, d, (SIB,), e)
 
     @pl.when(jnp.logical_not(owner))
     def _():
@@ -363,18 +381,26 @@
     @pl.when(jnp.logical_not(owner))
     def _():
         h_sib.start()
-        near_copy(d, UP).wait_recv()
-        spread(near_copy, d, (UP, DOWN))
-
-    give_load.wait()
-    oy_copy = remote(ostage, go.at[d, k, y], oy_send.at[0], oy_recv.at[0], {"tp": across})
-    oy_copy.start()
+        for e in range(2):
+            near_copy(d, UP, e).wait_recv()
+            spread(near_copy, d, (UP, DOWN), e)
+
+    oy_copies = []
+    for e in range(2):
+        give_loads[e].wait()
+        oy_copies.append(
+            remote(
+                ostage.at[e], go.at[d, k, e, y], oy_send.at[e], oy_recv.at[e], {"tp": across}
+            )
+        )
+        oy_copies[e].start()
 
     def positions_of(shard, index):
         low = order[2 * shard] * half
         high = order[2 * shard + 1] * half
         return jnp.where(index < half, low + index, high + index - half)
 
+    order_load.wait()
     turn_load.wait()
     place = positions_of(k, lax.broadcasted_iota(jnp.int32, (rows, HEAD_SIZE), 0)).astype(F32)
     angle = place * turns[...]
@@ -390,8 +416,9 @@
     def _():
         h_x.start()
 
-    far_copy(d, UP).wait_recv()
-    spread(far_copy, d, (UP, DOWN, SIB))
+    for e in range(2):
+        far_copy(d, UP, e).wait_recv()
+        spread(far_copy, d, (UP, DOWN, SIB), e)
 
     for s in range(2, nd - 1):
         relay(near_copy, s)
@@ -427,11 +454,12 @@
     for s in range(2, nd - 1):
         relay(far_copy, s)
 
-    keep_load.wait()
-    remote(
-        ostage, go.at[d, k, 1 - y], oy_send.at[0], oy_recv.at[0], {"tp": across}
-    ).wait_recv()
-    spread(o_copy, d, (UP, DOWN, SIB))
+    for e in range(2):
+        keep_loads[e].wait()
+        remote(
+            ostage.at[e], go.at[d, k, e, 1 - y], oy_send.at[e], oy_recv.at[e], {"tp": across}
+        ).wait_recv()
+        spread(o_copy, d, (UP, DOWN, SIB), e)
 
     @pl.when(owner)
     def _():
@@ -474,10 +502,10 @@
 
         @pl.when(jnp.logical_not(owner & (b == b_own)))
         def _():
-            a_copy(line, i, SIB, 1 - k).wait_recv()
-
-        weights = ga[b].reshape(deep, ga.shape[3])
-        acc[...] += jnp.dot(normed[b], weights, preferred_element_type=F32)
+            for e in range(2):
+                a_copy(line, i, SIB, e, 1 - k).wait_recv()
+
+        acc[...] += jnp.dot(normed[b], ga[b], preferred_element_type=F32)
 
     def project_step(i, carry):
         @pl.when(i == nd - 1)
@@ -587,117 +615,113 @@
     js = nd // 2
     orow = min(256, rows)
 
-    def made_copy(i):
+    def made_copy(i, e):
         slot = (i % js) * 2 + y
         where = {"ctx": k, "tp": c * 2 + i // js}
-        return remote(made.at[i], arrived.at[slot], r_send.at[i], r_recv.at[slot], where)
+        return remote(
+            made.at[i, e], arrived.at[slot, e], r_send.at[i, e], r_recv.at[slot, e], where
+        )
 
     def stays(i):
         return (k == c) & (y == c) & (i // js == k)
 
     def out_step(n, carry):
-        @pl.when(n == nd - 1)
-        def _():
-            relay(o_copy, nd - 1)
-
-        i = nearest(n)
-        o_copy(i, SIB, 1 - k).wait_recv()
+        i, e = nearest(n // 2), n % 2
+
+        @pl.when(n >= 2 * (nd - 1))
+        def _():
+            relay(o_copy, nd - 1, (e,))
+
+        o_copy(i, SIB, e, 1 - k).wait_recv()
 
         def out_rows(m, inner):
             rr = pl.ds(pl.multiple_of(m * orow, orow), orow)
-            total = jnp.zeros((orow, hc), F32)
+            total = jnp.zeros((orow, hq), F32)
             for g in range(tp):
                 full = jnp.concatenate(
                     [attn[g * n_heads + h, rr, :] for h in range(n_heads)], axis=1
                 )
-                term = jnp.dot(full, go[i, g % 2, g // 2], preferred_element_type=F32)
+                term = jnp.dot(full, go[i, g % 2, e, g // 2], preferred_element_type=F32)
                 total = total + term.astype(BF16).astype(F32)
-            made[i, rr, :] = total.astype(BF16)
+            made[i, e, rr, :] = total.astype(BF16)
             return inner
 
         lax.fori_loop(0, rows // orow, out_rows, 0)
 
         @pl.when(jnp.logical_not(stays(i)))
         def _():
-            made_copy(i).start()
+            made_copy(i, e).start()
 
         @pl.when(stays(i))
         def _():
-            arrived[(i % js) * 2 + y] = made[i]
-
-        return carry
-
-    lax.fori_loop(0, nd, out_step, 0)
+            arrived[(i % js) * 2 + y, e] = made[i, e]
+
+        return carry
+
+    lax.fori_loop(0, 2 * nd, out_step, 0)
     goal_load.wait()
     tile[...] = jnp.zeros_like(tile)
 
-    def out_copy(slot):
-        place = pl.ds(pl.multiple_of(slot * hc, hc), hc)
-        return pltpu.make_async_copy(arrived.at[slot], out.at[:, place], out_sem.at[slot])
+    last = min(256, rows)
 
     def finish_block(n, carry):
-        j = jnp.where(d < nd // 2, n // 2, js - 1 - n // 2)
-        side = n % 2
+        j = jnp.where(d < nd // 2, n // 4, js - 1 - n // 4)
+        e, side = n // 2 % 2, n % 2
         slot = j * 2 + side
 
         @pl.when(jnp.logical_not((y == c) & (side == y) & (c == k)))
         def _():
             remote(
-                made.at[0], arrived.at[slot], r_send.at[0], r_recv.at[slot], {"tp": sibling}
+                made.at[0, 0], arrived.at[slot, e], r_send.at[0, 0], r_recv.at[slot, e],
+                {"tp": sibling},
             ).wait_recv()
 
-        out_copy(slot).start()
-        place = pl.ds(pl.multiple_of(slot * hc, hc), hc)
+        place = pl.ds(pl.multiple_of(slot * hc + e * hq, hq), hq)
 
         def finish(i, inner):
-            rr = pl.ds(pl.multiple_of(i * chunk, chunk), chunk)
-            result = arrived[slot, rr, :]
+            rr = pl.ds(pl.multiple_of(i * last, last), last)
+            result = arrived[slot, e, rr, :]
+            out[rr, place] = result
             resid = mine[rr, place].astype(F32) + result.astype(F32)
             resid = resid - goal[rr, place].astype(F32)
-            sq = jnp.sum((resid * resid).reshape(chunk // 8, 8, hc), axis=0)
-            part = sq[:, 0:128]
-            for m in range(1, hc // 128):
-                part = part + sq[:, m * 128 : (m + 1) * 128]
-            tile[...] += part
+            tile[...] += jnp.sum((resid * resid).reshape(last // 8, 8, hq), axis=0)
             return inner
 
-        lax.fori_loop(0, rows // chunk, finish, 0)
-        return carry
-
-    lax.fori_loop(0, 2 * js, finish_block, 0)
+        lax.fori_loop(0, rows // last, finish, 0)
+        return carry
+
+    lax.fori_loop(0, 4 * js, finish_block, 0)
 
     everyone = plane * nd
     number = d * plane + seat
 
-    def l_copy(s, slot):
+    def l_copy(s):
         p = (number + s) % everyone
         return remote(
-            sums.at[slot], sums.at[slot], l_send.at[s], l_recv.at[slot],
+            sums.at[number], sums.at[number], l_send.at[0], l_recv.at[0],
             {"ctx": p % plane // tp, "tp": p % tp, "dp": p // plane},
         )
 
+    others = sums.at[pl.ds(0, everyone - 1)]
+    l_all = remote(others, others, l_send.at[0], l_recv.at[0], {"tp": sibling})
     sums[number] = tile[...]
 
     def share(s, carry):
-        l_copy(s, number).start()
+        l_copy(s).start()
         return carry
 
     lax.fori_loop(1, everyone, share, 0)
-
-    def collect(s, carry):
-        l_copy(s, (number + s) % everyone).wait_recv()
-        return carry
-
-    lax.fori_loop(1, everyone, collect, 0)
+    l_all.wait_recv()
     whole = sums[0]
     for b in range(1, everyone):
         whole = whole + sums[b]
     count = plane * nd * rows * wide
-    loss[0, 0] = jnp.sum(whole) / count
+    loss[...] = jnp.full(loss.shape, jnp.sum(whole) / count, F32)
 
     @pl.when(owner)
     def _():
-        half_copy.wait_send()
+        for copy in half_copies:
+            copy.wait_send()
 
     @pl.when(jnp.logical_not(owner))
     def _():
@@ -705,12 +729,11 @@
             copy.wait_send()
         h_sib.wait_send()
 
-    for slot in range(2 * js):
-        out_copy(slot).wait()
     h_y.wait_send()
     h_x.wait_send()
     h_relay_x.wait_send()
-    oy_copy.wait_send()
+    for copy in oy_copies:
+        copy.wait_send()
     kv_copy.wait_send()
 
     def drain_heads(h, carry):
@@ -727,35 +750,33 @@
 
     lax.fori_loop(0, early, drain_relays, 0)
 
-    def drain_line(i, carry):
+    def drain_line(n, carry):
+        i, e = n // 2, n % 2
+
         @pl.when(owner | (i != d))
         def _():
-            near_copy(i, SIB).wait_send()
-
-        far_copy(i, SIB).wait_send()
-        o_copy(i, SIB).wait_send()
+            near_copy(i, SIB, e).wait_send()
+
+        far_copy(i, SIB, e).wait_send()
+        o_copy(i, SIB, e).wait_send()
         for copy in (near_copy, far_copy, o_copy):
 
             @pl.when(up & (i <= d))
             def _():
-                copy(i, UP).wait_send()
+                copy(i, UP, e).wait_send()
 
             @pl.when(down & (i >= d))
             def _():
-                copy(i, DOWN).wait_send()
+                copy(i, DOWN, e).wait_send()
 
         @pl.when(jnp.logical_not(stays(i)))
         def _():
-            made_copy(i).wait_send()
-
-        return carry
-
-    lax.fori_loop(0, nd, drain_line, 0)
-    def drain_sums(s, carry):
-        l_copy(s, number).wait_send()
-        return carry
-
-    lax.fori_loop(1, everyone, drain_sums, 0)
+            made_copy(i, e).wait_send()
+
+        return carry
+
+    lax.fori_loop(0, 2 * nd, drain_line, 0)
+    l_all.wait_send()
 
 
 def fused(nd, hidden, target, gain, w_query, w_key, value_matrix, w_out, block_order):
@@ -767,21 +788,23 @@
     all_cols = qcols + w_key.shape[1] + value_matrix.shape[1]
     orows, ocols = w_out.shape
     hc = ocols // 2
+    order_shape = block_order.shape
     half = HEAD_SIZE // 2
     freqs = np.float64(rope_base) ** (-np.arange(half) * 2.0 / HEAD_SIZE)
     freqs = jnp.asarray(np.concatenate([freqs, freqs])[None, :].astype(np.float32))
     heads = qcols // HEAD_SIZE
     js = nd // 2
-    anyspace = pl.BlockSpec(memory_space=pl.ANY)
+    anyspace = pl.BlockSpec(memory_space=pltpu.HBM)
+    vmem = pl.BlockSpec(memory_space=pltpu.VMEM)
     dma = pltpu.SemaphoreType.DMA
     branch, loss = pl.pallas_call(
         functools.partial(layer, nd),
         out_shape=(
             jax.ShapeDtypeStruct((rows, wide), BF16),
-            jax.ShapeDtypeStruct((1, 1), F32),
+            jax.ShapeDtypeStruct((1, 128), F32),
         ),
         in_specs=[
-            pl.BlockSpec(memory_space=pltpu.SMEM),
+            anyspace,
             anyspace,
             anyspace,
             anyspace,
@@ -791,12 +814,12 @@
             anyspace,
             anyspace,
         ],
-        out_specs=(anyspace, pl.BlockSpec(memory_space=pltpu.SMEM)),
+        out_specs=(vmem, vmem),
         scratch_shapes=[
-            pltpu.VMEM((nb, 2, deep // 2, all_cols), BF16),
-            pltpu.VMEM((2, deep // 2, all_cols), BF16),
-            pltpu.VMEM((nd, 2, 2, orows, hc), BF16),
-            pltpu.VMEM((orows, hc), BF16),
+            pltpu.VMEM((nb, deep, all_cols), BF16),
+            pltpu.VMEM((deep, all_cols), BF16),
+            pltpu.VMEM((nd, 2, 2, 2, orows, hc // 2), BF16),
+            pltpu.VMEM((2, orows, hc // 2), BF16),
             pltpu.VMEM((rows, wide), BF16),
             pltpu.VMEM((tp, rows, wide), BF16),
             pltpu.VMEM((rows, wide), BF16),
@@ -806,47 +829,52 @@
             pltpu.VMEM((heads, rows, HEAD_SIZE), BF16),
             pltpu.VMEM((2, rows, 2 * HEAD_SIZE), BF16),
             pltpu.VMEM((tp * heads, rows, HEAD_SIZE), BF16),
-            pltpu.VMEM((nd, rows, hc), BF16),
-            pltpu.VMEM((2 * js, rows, hc), BF16),
-            pltpu.VMEM((8, 128), F32),
-            pltpu.VMEM((plane * nd, 8, 128), F32),
+            pltpu.VMEM((nd, 2, rows, hc // 2), BF16),
+            pltpu.VMEM((2 * js, 2, rows, hc // 2), BF16),
+            pltpu.VMEM((8, hc // 2), F32),
+            pltpu.VMEM((plane * nd, 8, hc // 2), F32),
             pltpu.VMEM((1, tp * wide), F32),
             pltpu.VMEM((1, HEAD_SIZE), F32),
+            pltpu.SMEM(order_shape, jnp.int32),
             dma((13,)),
-            dma((2 * js,)),
-            dma((3,)),
-            dma((3, nb)),
+            dma((6,)),
+            dma((3, nb, 2)),
+            dma((nb, 4)),
+            dma((2,)),
+            dma((2,)),
+            dma((3, nd, 2)),
             dma((nb, 2)),
-            dma((1,)),
-            dma((1,)),
-            dma((3, nd)),
-            dma((nb,)),
             dma((4,)),
             dma((tp,)),
             dma((1,)),
             dma((1,)),
             dma((2, 2 * heads)),
             dma((tp * heads,)),
-            dma((nd,)),
-            dma((2 * js,)),
-            dma((plane * nd,)),
-            dma((plane * nd,)),
+            dma((nd, 2)),
+            dma((2 * js, 2)),
+            dma((1,)),
+            dma((1,)),
         ],
         compiler_params=pltpu.CompilerParams(
-            collective_id=1, has_side_effects=True, vmem_limit_bytes=60 * 1024 * 1024
+            collective_id=1, has_side_effects=True, vmem_limit_bytes=36 * 1024 * 1024
         ),
     )(
-        block_order,
-        hidden[0],
-        target[0],
-        gain[None, :],
-        freqs,
-        w_query,
-        w_key,
-        value_matrix,
-        w_out,
-    )
-    return (branch[None], loss.reshape(()))
+        *(
+            pltpu.with_memory_space_constraint(v, pltpu.HBM)
+            for v in (
+                block_order,
+                hidden[0],
+                target[0],
+                gain[None, :],
+                freqs,
+                w_query,
+                w_key,
+                value_matrix,
+                w_out,
+            )
+        )
+    )
+    return (branch[None], loss[0, 0])
 
 
 def solution(mesh):

time: 114 us -> 108 us (0.947)
  Pallas kernels: 109 us -> 105 us
  local copies, waits for them, and re-layouts: 2.26 us -> 0.97 us
    pallas_call x1, Pallas kernels: 109 us -> 105 us  [fused(): pl.pallas_call(functools.partial(layer, nd), out_shape=(jax.ShapeDtypeStr...]
    unnamed x1, local copies, waits for them, and re-layouts: 2.26 us -> 0.97 us
where the time goes in v3:
time: 108 us
  Pallas kernels  105 us (97%)
  between operations  1.81 us (2%)
    pallas_call x1, Pallas kernels, fused(): pl.pallas_call(functools.partial(layer, nd), out_shape=(jax.ShapeDtypeStr...  105 us

profile of v3, /device:TPU:0, one launch (start us, length us, event | category | flops | bytes accessed | tf_op | source)
XLA Modules:
  0.0 107.8 jit_solution(9225094041519391785)
XLA Ops:
  0.6 105.0 %shard_map.104 = (bf16[512,1024]{1,0:T(8,128)(2,1)S(1)}, f32[1,128]{1,0:T(1,128)S(1)}) custom-call(s32[4]{0:T(128)} %order_in.1, bf16[512,1024]{1,0:T(8,128)(2,1)} %bitcast.8, bf16[512,1024]{1,0:T(8,128)(2,1)} %bitcast.9, f32[1,4096]{1,0:T(1,128)} %bitcast.10, f32[1,128]{1,0:T(1,128)} %constant.2.clone.freqs, bf16[512,512]{1,0:T(8,128)(2,1)} %w_query.1, ...), custom_call_target="tpu_custom_call" | custom-call | tf_op jit(solution)/shard_map/pallas_call | solution.py:800
  105.7 1.0 copy.13

commit v4 on v3

--- a/solution.py
+++ b/solution.py
@@ -167,6 +167,7 @@
     attn,
     made,
     arrived,
+    want,
     tile,
     sums,
     gains,
@@ -176,6 +177,7 @@
     x_send,
     a_send,
     a_recv,
+    sib_recv,
     oy_send,
     oy_recv,
     o_send,
@@ -188,6 +190,8 @@
     at_recv,
     r_send,
     r_recv,
+    w_send,
+    w_recv,
     l_send,
     l_recv,
 ):
@@ -229,7 +233,7 @@
         return pl.ds(pl.multiple_of(half_of * hc + part * hq, hq), hq)
 
     keep_loads = [
-        load(4 + e, w_out.at[:, columns_of(y, e)], go.at[d, k, e, y]) for e in range(2)
+        load(4 + e, w_out.at[:, columns_of(y, e)], go.at[d * 2 + k, e, y]) for e in range(2)
     ]
     give_loads = [
         load(6 + e, w_out.at[:, columns_of(1 - y, e)], ostage.at[e]) for e in range(2)
@@ -294,15 +298,15 @@
         }[way]
 
     def a_copy(line, i, way, e, core=k):
-        b, piece = line * nd + i, 2 * core + e
-        ref = ga.at[b, rows_of(piece)]
-        return remote(ref, ref, a_send.at[way, b, e], a_recv.at[b, piece], target_of(way))
+        b = line * nd + i
+        ref = ga.at[b, rows_of(2 * core + e)]
+        there = sib_recv.at[b] if way == SIB else a_recv.at[b, e]
+        return remote(ref, ref, a_send.at[int(way == SIB)], there, target_of(way))
 
     def o_copy(i, way, e, core=k):
-        ref = go.at[i, core, e]
-        return remote(
-            ref, ref, o_send.at[way, i, e], o_recv.at[core * nd + i, e], target_of(way)
-        )
+        ref = go.at[i * 2 + core, e]
+        there = o_recv.at[core * nd + i, e]
+        return remote(ref, ref, o_send.at[int(way == SIB)], there, target_of(way))
 
     def spread(copy, i, ways, e):
         copy_up = lambda: copy(i, UP, e).start()
@@ -336,7 +340,7 @@
         ref = ga.at[b_own, rows_of(2 * (1 - k) + e)]
         half_copies.append(
             remote(
-                ref, ref, x_send.at[4 + e], a_recv.at[b_own, 2 * (1 - k) + e], {"tp": sibling}
+                ref, ref, x_send.at[0], a_recv.at[b_own, e], {"tp": sibling}
             )
         )
         for h in range(2):
@@ -345,8 +349,8 @@
                 remote(
                     stage.at[rows_of(piece)],
                     ga.at[b_own, rows_of(piece)],
-                    x_send.at[piece],
-                    a_recv.at[b_own, piece],
+                    x_send.at[0],
+                    a_recv.at[b_own, e],
                     {"ctx": 1 - c, "tp": y * 2 + h},
                 )
             )
@@ -390,7 +394,7 @@
         give_loads[e].wait()
         oy_copies.append(
             remote(
-                ostage.at[e], go.at[d, k, e, y], oy_send.at[e], oy_recv.at[e], {"tp": across}
+                ostage.at[e], go.at[d * 2 + k, e, y], oy_send.at[0], oy_recv.at[e], {"tp": across}
             )
         )
         oy_copies[e].start()
@@ -457,7 +461,7 @@
     for e in range(2):
         keep_loads[e].wait()
         remote(
-            ostage.at[e], go.at[d, k, e, 1 - y], oy_send.at[e], oy_recv.at[e], {"tp": across}
+            ostage.at[e], go.at[d * 2 + k, e, 1 - y], oy_send.at[0], oy_recv.at[e], {"tp": across}
         ).wait_recv()
         spread(o_copy, d, (UP, DOWN, SIB), e)
 
@@ -472,6 +476,32 @@
         h_wait(y * 2 + 1)
         h_wait(far)
         h_wait(far + 1)
+
+    js = nd // 2
+    keeps = (k == c) & (y == c)
+
+    def slot_columns(slot):
+        return pl.ds(pl.multiple_of(slot * hc, hc), hc)
+
+    def nearest(i):
+        return jnp.where(d < nd // 2, i, nd - 1 - i)
+
+    last = nearest(nd - 1)
+    last_j, last_core = last % js, last // js
+    ships = k == last_core
+
+    def want_copy(side):
+        return remote(
+            goal.at[:, slot_columns(last_j * 2 + side)],
+            want,
+            w_send.at[0],
+            w_recv.at[0],
+            {"ctx": y, "tp": side * 2 + c},
+        )
+
+    keep_want = pltpu.make_async_copy(
+        target.at[:, slot_columns(last_j * 2 + y)], want, w_recv.at[0]
+    )
 
     gain_load.wait()
     chunk = min(64, rows)
@@ -492,18 +522,27 @@
         return carry
 
     lax.fori_loop(0, rows // chunk, norm_rows, 0)
+    goal_load.wait()
+
+    @pl.when(keeps & ships)
+    def _():
+        keep_want.start()
+
+    for side in range(2):
+
+        @pl.when(ships & jnp.logical_not(keeps & (side == y)))
+        def _():
+            want_copy(side).start()
+
     acc[...] = jnp.zeros_like(acc)
-
-    def nearest(i):
-        return jnp.where(d < nd // 2, i, nd - 1 - i)
 
     def project(i, line):
         b = line * nd + i
 
         @pl.when(jnp.logical_not(owner & (b == b_own)))
         def _():
-            for e in range(2):
-                a_copy(line, i, SIB, e, 1 - k).wait_recv()
+            ref = ga.at[b, pl.ds(0, deep // 2)]
+            remote(ref, ref, a_send.at[1], sib_recv.at[b], {"tp": sibling}).wait_recv()
 
         acc[...] += jnp.dot(normed[b], ga[b], preferred_element_type=F32)
 
@@ -540,11 +579,17 @@
     spots = ({"ctx": 1 - c}, {"tp": across})
     x_group, y_group = y * 2 + 1 - c, (1 - y) * 2 + c
 
+    early = n_heads // 2
+
     def at_copy(h, way, source=group):
-        b = source * n_heads + h
-        ref = attn.at[b]
-        sem = at_send.at[way, jnp.where(source == group, 0, n_heads) + h]
-        return remote(ref, ref, sem, at_recv.at[b], spots[way])
+        ref = attn.at[source * n_heads + h]
+        first = h < early if way == 0 else h >= early
+        there = jnp.where(first & (source == group), h, n_heads)
+        return remote(ref, ref, at_send.at[0], at_recv.at[there], spots[way])
+
+    def at_arrival(h, source):
+        ref = attn.at[source * n_heads + h]
+        return remote(ref, ref, at_send.at[0], at_recv.at[h], spots[0])
 
     def attend_head(h, carry):
         def attend_block(i, inner):
@@ -583,12 +628,10 @@
     for s in range(1, min(2, nd - 1)):
         relay(o_copy, s)
 
-    early = n_heads // 2
-
     def at_relay(h, carry):
-        at_copy(h, 0, x_group).wait_recv()
+        at_arrival(h, x_group).wait_recv()
         at_copy(h, 1, x_group).start()
-        at_copy(early + h, 1, y_group).wait_recv()
+        at_arrival(early + h, y_group).wait_recv()
         at_copy(early + h, 0, y_group).start()
         return carry
 
@@ -597,120 +640,175 @@
     for s in range(2, nd - 1):
         relay(o_copy, s)
 
-
-    def at_wait(h, carry):
-        at_copy(early + h, 0, x_group).wait_recv()
-        at_copy(h, 1, y_group).wait_recv()
-        return carry
-
-    lax.fori_loop(0, early, at_wait, 0)
-    z_group = (1 - y) * 2 + 1 - c
-
-    def far_wait(h, carry):
-        at_copy(h, 1, z_group).wait_recv()
-        return carry
-
-    lax.fori_loop(0, n_heads, far_wait, 0)
-
-    js = nd // 2
+    rest = attn.at[pl.ds(0, 2 * n_heads)]
+    remote(rest, rest, at_send.at[0], at_recv.at[n_heads], spots[0]).wait_recv()
+
     orow = min(256, rows)
 
-    def made_copy(i, e):
+    def made_copy(i, e, rr):
         slot = (i % js) * 2 + y
         where = {"ctx": k, "tp": c * 2 + i // js}
         return remote(
-            made.at[i, e], arrived.at[slot, e], r_send.at[i, e], r_recv.at[slot, e], where
+            made.at[i, e, rr], arrived.at[slot, e, rr], r_send.at[0], r_recv.at[slot, e], where
         )
 
     def stays(i):
-        return (k == c) & (y == c) & (i // js == k)
-
-    def out_step(n, carry):
-        i, e = nearest(n // 2), n % 2
-
-        @pl.when(n >= 2 * (nd - 1))
-        def _():
-            relay(o_copy, nd - 1, (e,))
-
-        o_copy(i, SIB, e, 1 - k).wait_recv()
-
-        def out_rows(m, inner):
-            rr = pl.ds(pl.multiple_of(m * orow, orow), orow)
-            total = jnp.zeros((orow, hq), F32)
-            for g in range(tp):
-                full = jnp.concatenate(
-                    [attn[g * n_heads + h, rr, :] for h in range(n_heads)], axis=1
-                )
-                term = jnp.dot(full, go[i, g % 2, e, g // 2], preferred_element_type=F32)
-                total = total + term.astype(BF16).astype(F32)
-            made[i, e, rr, :] = total.astype(BF16)
-            return inner
-
-        lax.fori_loop(0, rows // orow, out_rows, 0)
-
+        return keeps & (i // js == k)
+
+    def gathered(g, rr):
+        return jnp.concatenate([attn[g * n_heads + h, rr, :] for h in range(n_heads)], axis=1)
+
+    tile[...] = jnp.zeros_like(tile)
+
+    def keep_or_send(i, e, rr, value, final):
         @pl.when(jnp.logical_not(stays(i)))
         def _():
-            made_copy(i, e).start()
+            made[i, e, rr, :] = value
+            made_copy(i, e, rr).start()
 
         @pl.when(stays(i))
         def _():
-            arrived[(i % js) * 2 + y, e] = made[i, e]
-
+            arrived[(i % js) * 2 + y, e, rr, :] = value
+
+        if not final:
+            return
+        spot = pl.ds(pl.multiple_of(((i % js) * 2 + y) * hc + e * hq, hq), hq)
+        part = pl.ds(pl.multiple_of(e * hq, hq), hq)
+        resid = xs[c * 2 + i // js, rr, spot].astype(F32) + value.astype(F32)
+        resid = resid - want[rr, part].astype(F32)
+        tile[...] += jnp.sum((resid * resid).reshape(orow // 8, 8, hq), axis=0)
+
+    def rows_at(m):
+        return pl.ds(pl.multiple_of(m * orow, orow), orow)
+
+    def whole_block(n, carry):
+        i = nearest(n)
+        for e in range(2):
+            o_copy(i, SIB, e, 1 - k).wait_recv()
+
+        def all_rows(m, inner):
+            rr = rows_at(m)
+            total = jnp.zeros((orow, hc), F32)
+            for g in range(tp):
+                b = i * 2 + g % 2
+                weights = jnp.concatenate([go[b, e, g // 2] for e in range(2)], axis=1)
+                term = jnp.dot(gathered(g, rr), weights, preferred_element_type=F32)
+                total = total + term.astype(BF16).astype(F32)
+            for e in range(2):
+                keep_or_send(i, e, rr, total[:, e * hq : (e + 1) * hq].astype(BF16), False)
+            return inner
+
+        lax.fori_loop(0, rows // orow, all_rows, 0)
         return carry
 
-    lax.fori_loop(0, 2 * nd, out_step, 0)
-    goal_load.wait()
-    tile[...] = jnp.zeros_like(tile)
-
-    last = min(256, rows)
-
-    def finish_block(n, carry):
+    lax.fori_loop(0, nd - 1, whole_block, 0)
+
+    def finish_block(squares, n, carry):
         j = jnp.where(d < nd // 2, n // 4, js - 1 - n // 4)
         e, side = n // 2 % 2, n % 2
         slot = j * 2 + side
 
-        @pl.when(jnp.logical_not((y == c) & (side == y) & (c == k)))
+        @pl.when(jnp.logical_not(keeps & (side == y)))
         def _():
             remote(
-                made.at[0, 0], arrived.at[slot, e], r_send.at[0, 0], r_recv.at[slot, e],
+                made.at[0, 0], arrived.at[slot, e], r_send.at[0], r_recv.at[slot, e],
                 {"tp": sibling},
             ).wait_recv()
 
         place = pl.ds(pl.multiple_of(slot * hc + e * hq, hq), hq)
-
-        def finish(i, inner):
-            rr = pl.ds(pl.multiple_of(i * last, last), last)
+        if not squares:
+            out[:, place] = arrived[slot, e]
+            return carry
+
+        def finish(m, inner):
+            rr = rows_at(m)
             result = arrived[slot, e, rr, :]
             out[rr, place] = result
             resid = mine[rr, place].astype(F32) + result.astype(F32)
             resid = resid - goal[rr, place].astype(F32)
-            tile[...] += jnp.sum((resid * resid).reshape(last // 8, 8, hq), axis=0)
+            tile[...] += jnp.sum((resid * resid).reshape(orow // 8, 8, hq), axis=0)
             return inner
 
-        lax.fori_loop(0, rows // last, finish, 0)
+        lax.fori_loop(0, rows // orow, finish, 0)
         return carry
 
-    lax.fori_loop(0, 4 * js, finish_block, 0)
+    def half_block(e, carry):
+        i = nearest(nd - 1)
+        relay(o_copy, nd - 1, (e,))
+
+        def terms(core, rr):
+            total = jnp.zeros((orow, hq), F32)
+            for side in range(2):
+                weights = go[i * 2 + core, e, side]
+                term = jnp.dot(
+                    gathered(2 * side + core, rr), weights, preferred_element_type=F32
+                )
+                total = total + term.astype(BF16).astype(F32)
+            return total
+
+        def own_rows(m, inner):
+            acc[rows_at(m), 0:hq] = terms(k, rows_at(m))
+            return inner
+
+        lax.fori_loop(0, rows // orow, own_rows, 0)
+        o_copy(i, SIB, e, 1 - k).wait_recv()
+
+        def all_rows(m, inner):
+            rr = rows_at(m)
+            value = (acc[rr, 0:hq] + terms(1 - k, rr)).astype(BF16)
+            keep_or_send(i, e, rr, value, True)
+            return inner
+
+        lax.fori_loop(0, rows // orow, all_rows, 0)
+        return carry
+
+    early_end = jnp.where(ships, 0, 4 * js)
+    others_end = 4 * js - 4 * ships.astype(jnp.int32)
+
+
+    @pl.when(keeps & ships)
+    def _():
+        keep_want.wait()
+
+    @pl.when(jnp.logical_not(keeps & ships))
+    def _():
+        remote(want, want, w_send.at[0], w_recv.at[0], {"tp": sibling}).wait_recv()
+
+    def last_step(e, carry):
+        half_block(e, carry)
+
+        @pl.when(e == 0)
+        def _():
+            lax.fori_loop(0, early_end, functools.partial(finish_block, True), 0)
+
+        return carry
+
+    lax.fori_loop(0, 2, last_step, 0)
+    lax.fori_loop(early_end, others_end, functools.partial(finish_block, True), 0)
 
     everyone = plane * nd
     number = d * plane + seat
 
-    def l_copy(s):
-        p = (number + s) % everyone
+    def l_copy(n):
+        r = everyone - 1 - n
+        p = (seat + r) % plane
+        z = jnp.where(d < nd // 2, (d + r // plane) % nd, (d + nd - r // plane) % nd)
         return remote(
             sums.at[number], sums.at[number], l_send.at[0], l_recv.at[0],
-            {"ctx": p % plane // tp, "tp": p % tp, "dp": p // plane},
+            {"ctx": p // tp, "tp": p % tp, "dp": z},
         )
 
     others = sums.at[pl.ds(0, everyone - 1)]
     l_all = remote(others, others, l_send.at[0], l_recv.at[0], {"tp": sibling})
     sums[number] = tile[...]
 
-    def share(s, carry):
-        l_copy(s).start()
+    def share(n, carry):
+        l_copy(n).start()
         return carry
 
-    lax.fori_loop(1, everyone, share, 0)
+    lax.fori_loop(0, everyone - 1, share, 0)
+    lax.fori_loop(others_end, 4 * js, functools.partial(finish_block, False), 0)
+
     l_all.wait_recv()
     whole = sums[0]
     for b in range(1, everyone):
@@ -718,64 +816,53 @@
     count = plane * nd * rows * wide
     loss[...] = jnp.full(loss.shape, jnp.sum(whole) / count, F32)
 
+    def sent(ref, sem):
+        remote(ref, ref, sem, kv_recv.at[0], {"tp": sibling}).wait_send()
+
+    for line_at in range(nd):
+        blocks = (line_at + 1) * (line_at < nd - 1) + (nd - line_at) * (line_at > 0)
+
+        @pl.when(d == line_at)
+        def _():
+            sent(ga.at[pl.ds(0, blocks)], a_send.at[0])
+            sent(go.at[pl.ds(0, blocks)], o_send.at[0])
+
+    sent(go.at[pl.ds(0, nd)], o_send.at[1])
+
     @pl.when(owner)
     def _():
-        for copy in half_copies:
-            copy.wait_send()
+        sent(ga.at[0, pl.ds(0, deep // 2)], x_send.at[0])
+        sent(ga.at[pl.ds(0, nd)], a_send.at[1])
 
     @pl.when(jnp.logical_not(owner))
     def _():
-        for copy in x_copies:
-            copy.wait_send()
+        sent(ga.at[0], x_send.at[0])
+        sent(ga.at[pl.ds(0, 2 * nd - 1), pl.ds(0, deep // 2)], a_send.at[1])
         h_sib.wait_send()
 
     h_y.wait_send()
     h_x.wait_send()
     h_relay_x.wait_send()
-    for copy in oy_copies:
-        copy.wait_send()
+    sent(ostage, oy_send.at[0])
     kv_copy.wait_send()
-
-    def drain_heads(h, carry):
-        for way in range(2):
-            at_copy(h, way).wait_send()
-        return carry
-
-    lax.fori_loop(0, n_heads, drain_heads, 0)
-
-    def drain_relays(h, carry):
-        at_copy(h, 1, x_group).wait_send()
-        at_copy(early + h, 0, y_group).wait_send()
-        return carry
-
-    lax.fori_loop(0, early, drain_relays, 0)
-
-    def drain_line(n, carry):
-        i, e = n // 2, n % 2
-
-        @pl.when(owner | (i != d))
-        def _():
-            near_copy(i, SIB, e).wait_send()
-
-        far_copy(i, SIB, e).wait_send()
-        o_copy(i, SIB, e).wait_send()
-        for copy in (near_copy, far_copy, o_copy):
-
-            @pl.when(up & (i <= d))
-            def _():
-                copy(i, UP, e).wait_send()
-
-            @pl.when(down & (i >= d))
-            def _():
-                copy(i, DOWN, e).wait_send()
-
-        @pl.when(jnp.logical_not(stays(i)))
-        def _():
-            made_copy(i, e).wait_send()
-
-        return carry
-
-    lax.fori_loop(0, 2 * nd, drain_line, 0)
+    sent(attn.at[pl.ds(0, 3 * n_heads)], at_send.at[0])
+
+    @pl.when(keeps)
+    def _():
+        sent(made.at[pl.ds(0, nd - js)], r_send.at[0])
+
+    @pl.when(jnp.logical_not(keeps))
+    def _():
+        sent(made, r_send.at[0])
+
+    @pl.when(ships & keeps)
+    def _():
+        sent(want, w_send.at[0])
+
+    @pl.when(ships & jnp.logical_not(keeps))
+    def _():
+        sent(arrived.at[pl.ds(0, 2)], w_send.at[0])
+
     l_all.wait_send()
 
 
@@ -818,7 +905,7 @@
         scratch_shapes=[
             pltpu.VMEM((nb, deep, all_cols), BF16),
             pltpu.VMEM((deep, all_cols), BF16),
-            pltpu.VMEM((nd, 2, 2, 2, orows, hc // 2), BF16),
+            pltpu.VMEM((2 * nd, 2, 2, orows, hc // 2), BF16),
             pltpu.VMEM((2, orows, hc // 2), BF16),
             pltpu.VMEM((rows, wide), BF16),
             pltpu.VMEM((tp, rows, wide), BF16),
@@ -831,27 +918,31 @@
             pltpu.VMEM((tp * heads, rows, HEAD_SIZE), BF16),
             pltpu.VMEM((nd, 2, rows, hc // 2), BF16),
             pltpu.VMEM((2 * js, 2, rows, hc // 2), BF16),
+            pltpu.VMEM((rows, hc), BF16),
             pltpu.VMEM((8, hc // 2), F32),
             pltpu.VMEM((plane * nd, 8, hc // 2), F32),
             pltpu.VMEM((1, tp * wide), F32),
             pltpu.VMEM((1, HEAD_SIZE), F32),
             pltpu.SMEM(order_shape, jnp.int32),
             dma((13,)),
-            dma((6,)),
-            dma((3, nb, 2)),
-            dma((nb, 4)),
+            dma((1,)),
+            dma((2,)),
+            dma((nb, 2)),
+            dma((nb,)),
+            dma((1,)),
             dma((2,)),
             dma((2,)),
-            dma((3, nd, 2)),
             dma((nb, 2)),
             dma((4,)),
             dma((tp,)),
             dma((1,)),
             dma((1,)),
-            dma((2, 2 * heads)),
-            dma((tp * heads,)),
-            dma((nd, 2)),
+            dma((1,)),
+            dma((heads + 1,)),
+            dma((1,)),
             dma((2 * js, 2)),
+            dma((1,)),
+            dma((1,)),
             dma((1,)),
             dma((1,)),
         ],

time: 108 us -> 103 us (0.954)
  Pallas kernels: 105 us -> 100 us
    pallas_call x1, Pallas kernels: 105 us -> 100 us  [fused(): pl.pallas_call(functools.partial(layer, nd), out_shape=(jax.ShapeDtypeStr...]
where the time goes in v4:
time: 103 us
  Pallas kernels  100 us (97%)
  between operations  1.81 us (2%)
    pallas_call x1, Pallas kernels, fused(): pl.pallas_call(functools.partial(layer, nd), out_shape=(jax.ShapeDtypeStr...  100 us

profile of v4, /device:TPU:0, one launch (start us, length us, event | category | flops | bytes accessed | tf_op | source)
XLA Modules:
  0.0 102.9 jit_solution(14998224813001866201)
XLA Ops:
  0.6 100.2 %shard_map.104 = (bf16[512,1024]{1,0:T(8,128)(2,1)S(1)}, f32[1,128]{1,0:T(1,128)S(1)}) custom-call(s32[4]{0:T(128)} %order_in.1, bf16[512,1024]{1,0:T(8,128)(2,1)} %bitcast.8, bf16[512,1024]{1,0:T(8,128)(2,1)} %bitcast.9, f32[1,4096]{1,0:T(1,128)} %bitcast.10, f32[1,128]{1,0:T(1,128)} %constant.2.clone.freqs, bf16[512,512]{1,0:T(8,128)(2,1)} %w_query.1, ...), custom_call_target="tpu_custom_call" | custom-call | tf_op jit(solution)/shard_map/pallas_call | solution.py:887
  100.8 1.0 copy.13

commit v5 on v4

--- a/solution.py
+++ b/solution.py
@@ -269,18 +269,19 @@
 
     barrier = pltpu.get_barrier_semaphore()
     seat = c * tp + t
-    for s in range(1, plane):
-        p = (seat + s) % plane
-        pl.semaphore_signal(
-            barrier, inc=1, device_id={"ctx": p // tp, "tp": p % tp}, device_id_type=MESH
-        )
+    beside = [{"tp": sibling}]
+    for other in range(2):
+        beside += [{"ctx": 1 - c, "tp": y * 2 + other}, {"tp": (1 - y) * 2 + other}]
+    for where in beside:
+        pl.semaphore_signal(barrier, inc=1, device_id=where, device_id_type=MESH)
     for there, step in ((up, 1), (down, -1)):
 
         @pl.when(there)
         def _():
             pl.semaphore_signal(barrier, inc=1, device_id={"dp": d + step}, device_id_type=MESH)
 
-    pl.semaphore_wait(barrier, plane - 1 + up.astype(jnp.int32) + down.astype(jnp.int32))
+    near_count = len(beside) + up.astype(jnp.int32) + down.astype(jnp.int32)
+    pl.semaphore_wait(barrier, near_count)
 
     def remote(src, dst, ssem, rsem, where):
         return pltpu.make_async_remote_copy(

time: 103 us -> 103 us (level)
  no operation moved by 1% of the time
where the time goes in v5:
time: 103 us
  Pallas kernels  100 us (97%)
  between operations  1.81 us (2%)
    pallas_call x1, Pallas kernels, fused(): pl.pallas_call(functools.partial(layer, nd), out_shape=(jax.ShapeDtypeStr...  100 us

profile of v5, /device:TPU:0, one launch (start us, length us, event | category | flops | bytes accessed | tf_op | source)
XLA Modules:
  0.0 102.9 jit_solution(1605167230847714027)
XLA Ops:
  0.6 100.1 %shard_map.104 = (bf16[512,1024]{1,0:T(8,128)(2,1)S(1)}, f32[1,128]{1,0:T(1,128)S(1)}) custom-call(s32[4]{0:T(128)} %order_in.1, bf16[512,1024]{1,0:T(8,128)(2,1)} %bitcast.8, bf16[512,1024]{1,0:T(8,128)(2,1)} %bitcast.9, f32[1,4096]{1,0:T(1,128)} %bitcast.10, f32[1,128]{1,0:T(1,128)} %constant.2.clone.freqs, bf16[512,512]{1,0:T(8,128)(2,1)} %w_query.1, ...), custom_call_target="tpu_custom_call" | custom-call | tf_op jit(solution)/shard_map/pallas_call | solution.py:888
  100.8 1.0 copy.13

commit v6 on v5

--- a/solution.py
+++ b/solution.py
@@ -363,8 +363,6 @@
         for e in range(2):
             half_copies[e].start()
             spread(near_copy, d, (UP, DOWN), e)
-        for e in range(2):
-            spread(near_copy, d, (SIB,), e)
 
     @pl.when(jnp.logical_not(owner))
     def _():
@@ -385,7 +383,6 @@
 
     @pl.when(jnp.logical_not(owner))
     def _():
-        h_sib.start()
         for e in range(2):
             near_copy(d, UP, e).wait_recv()
             spread(near_copy, d, (UP, DOWN), e)
@@ -421,6 +418,15 @@
     def _():
         h_x.start()
 
+    @pl.when(owner)
+    def _():
+        for e in range(2):
+            spread(near_copy, d, (SIB,), e)
+
+    @pl.when(jnp.logical_not(owner))
+    def _():
+        h_sib.start()
+
     for e in range(2):
         far_copy(d, UP, e).wait_recv()
         spread(far_copy, d, (UP, DOWN, SIB), e)
@@ -488,21 +494,21 @@
         return jnp.where(d < nd // 2, i, nd - 1 - i)
 
     last = nearest(nd - 1)
-    last_j, last_core = last % js, last // js
-    ships = k == last_core
-
-    def want_copy(side):
+    ships = k == last // js
+
+    def want_copy(j, side):
         return remote(
-            goal.at[:, slot_columns(last_j * 2 + side)],
-            want,
+            goal.at[:, slot_columns(j * 2 + side)],
+            want.at[j],
             w_send.at[0],
-            w_recv.at[0],
+            w_recv.at[j],
             {"ctx": y, "tp": side * 2 + c},
         )
 
-    keep_want = pltpu.make_async_copy(
-        target.at[:, slot_columns(last_j * 2 + y)], want, w_recv.at[0]
-    )
+    def keep_want(j):
+        return pltpu.make_async_copy(
+            target.at[:, slot_columns(j * 2 + y)], want.at[j], w_recv.at[j]
+        )
 
     gain_load.wait()
     chunk = min(64, rows)
@@ -527,13 +533,15 @@
 
     @pl.when(keeps & ships)
     def _():
-        keep_want.start()
+        for j in range(js):
+            keep_want(j).start()
 
     for side in range(2):
 
         @pl.when(ships & jnp.logical_not(keeps & (side == y)))
         def _():
-            want_copy(side).start()
+            for j in range(js):
+                want_copy(j, side).start()
 
     acc[...] = jnp.zeros_like(acc)
 
@@ -676,14 +684,28 @@
         spot = pl.ds(pl.multiple_of(((i % js) * 2 + y) * hc + e * hq, hq), hq)
         part = pl.ds(pl.multiple_of(e * hq, hq), hq)
         resid = xs[c * 2 + i // js, rr, spot].astype(F32) + value.astype(F32)
-        resid = resid - want[rr, part].astype(F32)
+        resid = resid - want[i % js, rr, part].astype(F32)
         tile[...] += jnp.sum((resid * resid).reshape(orow // 8, 8, hq), axis=0)
 
     def rows_at(m):
         return pl.ds(pl.multiple_of(m * orow, orow), orow)
 
-    def whole_block(n, carry):
+    def want_wait(i):
+        @pl.when(keeps & ships)
+        def _():
+            keep_want(i % js).wait()
+
+        @pl.when(jnp.logical_not(keeps & ships))
+        def _():
+            ref = want.at[i % js]
+            remote(ref, ref, w_send.at[0], w_recv.at[i % js], {"tp": sibling}).wait_recv()
+
+    others_end = jnp.where(ships, 0, 4 * js)
+
+    def whole_block(final, n, carry):
         i = nearest(n)
+        if final:
+            want_wait(i)
         for e in range(2):
             o_copy(i, SIB, e, 1 - k).wait_recv()
 
@@ -696,13 +718,14 @@
                 term = jnp.dot(gathered(g, rr), weights, preferred_element_type=F32)
                 total = total + term.astype(BF16).astype(F32)
             for e in range(2):
-                keep_or_send(i, e, rr, total[:, e * hq : (e + 1) * hq].astype(BF16), False)
+                keep_or_send(i, e, rr, total[:, e * hq : (e + 1) * hq].astype(BF16), final)
             return inner
 
         lax.fori_loop(0, rows // orow, all_rows, 0)
         return carry
 
-    lax.fori_loop(0, nd - 1, whole_block, 0)
+    lax.fori_loop(0, js, functools.partial(whole_block, False), 0)
+    lax.fori_loop(js, nd - 1, functools.partial(whole_block, True), 0)
 
     def finish_block(squares, n, carry):
         j = jnp.where(d < nd // 2, n // 4, js - 1 - n // 4)
@@ -763,30 +786,19 @@
         lax.fori_loop(0, rows // orow, all_rows, 0)
         return carry
 
-    early_end = jnp.where(ships, 0, 4 * js)
-    others_end = 4 * js - 4 * ships.astype(jnp.int32)
-
-
-    @pl.when(keeps & ships)
-    def _():
-        keep_want.wait()
-
-    @pl.when(jnp.logical_not(keeps & ships))
-    def _():
-        remote(want, want, w_send.at[0], w_recv.at[0], {"tp": sibling}).wait_recv()
+
+    want_wait(last)
 
     def last_step(e, carry):
         half_block(e, carry)
 
         @pl.when(e == 0)
         def _():
-            lax.fori_loop(0, early_end, functools.partial(finish_block, True), 0)
+            lax.fori_loop(0, others_end, functools.partial(finish_block, True), 0)
 
         return carry
 
     lax.fori_loop(0, 2, last_step, 0)
-    lax.fori_loop(early_end, others_end, functools.partial(finish_block, True), 0)
-
     everyone = plane * nd
     number = d * plane + seat
 
@@ -801,13 +813,10 @@
 
     others = sums.at[pl.ds(0, everyone - 1)]
     l_all = remote(others, others, l_send.at[0], l_recv.at[0], {"tp": sibling})
-    sums[number] = tile[...]
-
-    def share(n, carry):
+    sums[number] = jnp.sum(tile[...], axis=0, keepdims=True)
+
+    for n in range(everyone - 1):
         l_copy(n).start()
-        return carry
-
-    lax.fori_loop(0, everyone - 1, share, 0)
     lax.fori_loop(others_end, 4 * js, functools.partial(finish_block, False), 0)
 
     l_all.wait_recv()
@@ -858,11 +867,11 @@
 
     @pl.when(ships & keeps)
     def _():
-        sent(want, w_send.at[0])
+        sent(arrived.at[pl.ds(0, js)], w_send.at[0])
 
     @pl.when(ships & jnp.logical_not(keeps))
     def _():
-        sent(arrived.at[pl.ds(0, 2)], w_send.at[0])
+        sent(arrived, w_send.at[0])
 
     l_all.wait_send()
 
@@ -919,9 +928,9 @@
             pltpu.VMEM((tp * heads, rows, HEAD_SIZE), BF16),
             pltpu.VMEM((nd, 2, rows, hc // 2), BF16),
             pltpu.VMEM((2 * js, 2, rows, hc // 2), BF16),
-            pltpu.VMEM((rows, hc), BF16),
+            pltpu.VMEM((js, rows, hc), BF16),
             pltpu.VMEM((8, hc // 2), F32),
-            pltpu.VMEM((plane * nd, 8, hc // 2), F32),
+            pltpu.VMEM((plane * nd, 1, hc // 2), F32),
             pltpu.VMEM((1, tp * wide), F32),
             pltpu.VMEM((1, HEAD_SIZE), F32),
             pltpu.SMEM(order_shape, jnp.int32),
@@ -943,7 +952,7 @@
             dma((1,)),
             dma((2 * js, 2)),
             dma((1,)),
-            dma((1,)),
+            dma((js,)),
             dma((1,)),
             dma((1,)),
         ],

time: 103 us -> 102 us (level)
  no operation moved by 1% of the time
where the time goes in v6:
time: 102 us
  Pallas kernels  99.5 us (98%)
  between operations  1.81 us (2%)
    pallas_call x1, Pallas kernels, fused(): pl.pallas_call(functools.partial(layer, nd), out_shape=(jax.ShapeDtypeStr...  99.5 us

profile of v6, /device:TPU:0, one launch (start us, length us, event | category | flops | bytes accessed | tf_op | source)
XLA Modules:
  0.0 102.2 jit_solution(17025040105304427287)
XLA Ops:
  0.6 99.5 %shard_map.104 = (bf16[512,1024]{1,0:T(8,128)(2,1)S(1)}, f32[1,128]{1,0:T(1,128)S(1)}) custom-call(s32[4]{0:T(128)} %order_in.1, bf16[512,1024]{1,0:T(8,128)(2,1)} %bitcast.8, bf16[512,1024]{1,0:T(8,128)(2,1)} %bitcast.9, f32[1,4096]{1,0:T(1,128)} %bitcast.10, f32[1,128]{1,0:T(1,128)} %constant.2.clone.freqs, bf16[512,512]{1,0:T(8,128)(2,1)} %w_query.1, ...), custom_call_target="tpu_custom_call" | custom-call | tf_op jit(solution)/shard_map/pallas_call | solution.py:897
  100.1 1.0 copy.13

commit v7 on v6

--- a/solution.py
+++ b/solution.py
@@ -824,7 +824,7 @@
     for b in range(1, everyone):
         whole = whole + sums[b]
     count = plane * nd * rows * wide
-    loss[...] = jnp.full(loss.shape, jnp.sum(whole) / count, F32)
+    loss[...] = whole / count
 
     def sent(ref, sem):
         remote(ref, ref, sem, kv_recv.at[0], {"tp": sibling}).wait_send()
@@ -898,7 +898,7 @@
         functools.partial(layer, nd),
         out_shape=(
             jax.ShapeDtypeStruct((rows, wide), BF16),
-            jax.ShapeDtypeStruct((1, 128), F32),
+            jax.ShapeDtypeStruct((1, hc // 2), F32),
         ),
         in_specs=[
             anyspace,
@@ -975,7 +975,7 @@
             )
         )
     )
-    return (branch[None], loss[0, 0])
+    return (branch[None], jnp.sum(loss))
 
 
 def solution(mesh):

time: 102 us -> 102 us (level)
  between operations: 1.81 us -> 0.64 us
where the time goes in v7:
time: 102 us
  Pallas kernels  99.3 us (97%)
    pallas_call x1, Pallas kernels, fused(): pl.pallas_call(functools.partial(layer, nd), out_shape=(jax.ShapeDtypeStr...  99.3 us

profile of v7, /device:TPU:0, one launch (start us, length us, event | category | flops | bytes accessed | tf_op | source)
XLA Modules:
  0.0 101.5 jit_solution(801255279756897597)
XLA Ops:
  0.6 99.3 %shard_map.104 = (bf16[512,1024]{1,0:T(8,128)(2,1)S(1)}, f32[1,128]{1,0:T(1,128)S(1)}) custom-call(s32[4]{0:T(128)} %order_in.1, bf16[512,1024]{1,0:T(8,128)(2,1)} %bitcast.5, bf16[512,1024]{1,0:T(8,128)(2,1)} %bitcast.6, f32[1,4096]{1,0:T(1,128)} %bitcast.7, f32[1,128]{1,0:T(1,128)} %constant.4.clone.freqs, bf16[512,512]{1,0:T(8,128)(2,1)} %w_query.1, ...), custom_call_target="tpu_custom_call" | custom-call | tf_op jit(solution)/shard_map/pallas_call | solution.py:897
  100.0 0.6 reduce_sum.9
  100.6 1.0 copy.12

commit v8 on v7

--- a/solution.py
+++ b/solution.py
@@ -373,8 +373,8 @@
 
     mine_load.wait()
     h_y = remote(mine, xs.at[t], h_send.at[0], h_recv.at[t], {"tp": (1 - y) * 2 + c})
-    h_x = remote(mine, xs.at[t], h_send.at[1], h_recv.at[t], {"ctx": 1 - c, "tp": y * 2 + c})
-    h_sib = remote(mine, xs.at[t], h_send.at[2], h_recv.at[t], {"tp": sibling})
+    h_x = remote(mine, xs.at[t], h_send.at[0], h_recv.at[t], {"ctx": 1 - c, "tp": y * 2 + c})
+    h_sib = remote(mine, xs.at[t], h_send.at[0], h_recv.at[t], {"tp": sibling})
     h_y.start()
 
     @pl.when(jnp.logical_not(owner) & (k == 0))
@@ -443,10 +443,10 @@
 
     far = (1 - y) * 2
     h_relay_x = remote(
-        xs.at[far + 1], xs.at[far + 1], h_send.at[3], h_recv.at[far + 1], {"ctx": 1 - c}
+        xs.at[far + 1], xs.at[far + 1], h_send.at[0], h_recv.at[far + 1], {"ctx": 1 - c}
     )
     h_relay_y = remote(
-        xs.at[y * 2], xs.at[y * 2], h_send.at[3], h_recv.at[y * 2], {"tp": across}
+        xs.at[y * 2], xs.at[y * 2], h_send.at[0], h_recv.at[y * 2], {"tp": across}
     )
 
     @pl.when(owner)
@@ -819,61 +819,59 @@
         l_copy(n).start()
     lax.fori_loop(others_end, 4 * js, functools.partial(finish_block, False), 0)
 
+    def sent(ref, sem):
+        remote(ref, ref, sem, kv_recv.at[0], {"tp": sibling}).wait_send()
+
+    for line_at in range(nd):
+        blocks = (line_at + 1) * (line_at < nd - 1) + (nd - line_at) * (line_at > 0)
+
+        @pl.when(d == line_at)
+        def _():
+            sent(ga.at[pl.ds(0, blocks)], a_send.at[0])
+            sent(go.at[pl.ds(0, blocks)], o_send.at[0])
+
+    sent(go.at[pl.ds(0, nd)], o_send.at[1])
+
+    @pl.when(owner)
+    def _():
+        sent(ga.at[0, pl.ds(0, deep // 2)], x_send.at[0])
+        sent(ga.at[pl.ds(0, nd)], a_send.at[1])
+        sent(xs.at[pl.ds(0, 3)], h_send.at[0])
+
+    @pl.when(jnp.logical_not(owner))
+    def _():
+        sent(ga.at[0], x_send.at[0])
+        sent(ga.at[pl.ds(0, 2 * nd - 1), pl.ds(0, deep // 2)], a_send.at[1])
+        sent(xs, h_send.at[0])
+
+    sent(ostage, oy_send.at[0])
+    kv_copy.wait_send()
+    sent(attn.at[pl.ds(0, 3 * n_heads)], at_send.at[0])
+
+    @pl.when(keeps)
+    def _():
+        sent(made.at[pl.ds(0, nd - js)], r_send.at[0])
+
+    @pl.when(jnp.logical_not(keeps))
+    def _():
+        sent(made, r_send.at[0])
+
+    @pl.when(ships & keeps)
+    def _():
+        sent(arrived.at[pl.ds(0, js)], w_send.at[0])
+
+    @pl.when(ships & jnp.logical_not(keeps))
+    def _():
+        sent(arrived, w_send.at[0])
+
+    l_all.wait_send()
+
     l_all.wait_recv()
     whole = sums[0]
     for b in range(1, everyone):
         whole = whole + sums[b]
     count = plane * nd * rows * wide
     loss[...] = whole / count
-
-    def sent(ref, sem):
-        remote(ref, ref, sem, kv_recv.at[0], {"tp": sibling}).wait_send()
-
-    for line_at in range(nd):
-        blocks = (line_at + 1) * (line_at < nd - 1) + (nd - line_at) * (line_at > 0)
-
-        @pl.when(d == line_at)
-        def _():
-            sent(ga.at[pl.ds(0, blocks)], a_send.at[0])
-            sent(go.at[pl.ds(0, blocks)], o_send.at[0])
-
-    sent(go.at[pl.ds(0, nd)], o_send.at[1])
-
-    @pl.when(owner)
-    def _():
-        sent(ga.at[0, pl.ds(0, deep // 2)], x_send.at[0])
-        sent(ga.at[pl.ds(0, nd)], a_send.at[1])
-
-    @pl.when(jnp.logical_not(owner))
-    def _():
-        sent(ga.at[0], x_send.at[0])
-        sent(ga.at[pl.ds(0, 2 * nd - 1), pl.ds(0, deep // 2)], a_send.at[1])
-        h_sib.wait_send()
-
-    h_y.wait_send()
-    h_x.wait_send()
-    h_relay_x.wait_send()
-    sent(ostage, oy_send.at[0])
-    kv_copy.wait_send()
-    sent(attn.at[pl.ds(0, 3 * n_heads)], at_send.at[0])
-
-    @pl.when(keeps)
-    def _():
-        sent(made.at[pl.ds(0, nd - js)], r_send.at[0])
-
-    @pl.when(jnp.logical_not(keeps))
-    def _():
-        sent(made, r_send.at[0])
-
-    @pl.when(ships & keeps)
-    def _():
-        sent(arrived.at[pl.ds(0, js)], w_send.at[0])
-
-    @pl.when(ships & jnp.logical_not(keeps))
-    def _():
-        sent(arrived, w_send.at[0])
-
-    l_all.wait_send()
 
 
 def fused(nd, hidden, target, gain, w_query, w_key, value_matrix, w_out, block_order):
@@ -943,7 +941,7 @@
             dma((2,)),
             dma((2,)),
             dma((nb, 2)),
-            dma((4,)),
+            dma((1,)),
             dma((tp,)),
             dma((1,)),
             dma((1,)),

time: 102 us -> 102 us (level)
  no operation moved by 1% of the time
where the time goes in v8:
time: 102 us; the launch traced here: 101 us
  Pallas kernels  99.3 us (97%)
    pallas_call x1, Pallas kernels, fused(): pl.pallas_call(functools.partial(layer, nd), out_shape=(jax.ShapeDtypeStr...  99.3 us

profile of v8, /device:TPU:0, one launch (start us, length us, event | category | flops | bytes accessed | tf_op | source)
XLA Modules:
  0.0 101.5 jit_solution(17512949917362426560)
XLA Ops:
  0.6 99.3 %shard_map.104 = (bf16[512,1024]{1,0:T(8,128)(2,1)S(1)}, f32[1,128]{1,0:T(1,128)S(1)}) custom-call(s32[4]{0:T(128)} %order_in.1, bf16[512,1024]{1,0:T(8,128)(2,1)} %bitcast.5, bf16[512,1024]{1,0:T(8,128)(2,1)} %bitcast.6, f32[1,4096]{1,0:T(1,128)} %bitcast.7, f32[1,128]{1,0:T(1,128)} %constant.4.clone.freqs, bf16[512,512]{1,0:T(8,128)(2,1)} %w_query.1, ...), custom_call_target="tpu_custom_call" | custom-call | tf_op jit(solution)/shard_map/pallas_call | solution.py:895
  99.9 0.6 reduce_sum.9
  100.5 1.0 copy.12

commit v9 on v8

--- a/solution.py
+++ b/solution.py
@@ -670,6 +670,13 @@
     tile[...] = jnp.zeros_like(tile)
 
     def keep_or_send(i, e, rr, value, final):
+        if final:
+            spot = pl.ds(pl.multiple_of(((i % js) * 2 + y) * hc + e * hq, hq), hq)
+            part = pl.ds(pl.multiple_of(e * hq, hq), hq)
+            resid = xs[c * 2 + i // js, rr, spot].astype(F32) + value.astype(F32)
+            resid = resid - want[i % js, rr, part].astype(F32)
+            tile[...] += jnp.sum((resid * resid).reshape(orow // 8, 8, hq), axis=0)
+
         @pl.when(jnp.logical_not(stays(i)))
         def _():
             made[i, e, rr, :] = value
@@ -678,14 +685,6 @@
         @pl.when(stays(i))
         def _():
             arrived[(i % js) * 2 + y, e, rr, :] = value
-
-        if not final:
-            return
-        spot = pl.ds(pl.multiple_of(((i % js) * 2 + y) * hc + e * hq, hq), hq)
-        part = pl.ds(pl.multiple_of(e * hq, hq), hq)
-        resid = xs[c * 2 + i // js, rr, spot].astype(F32) + value.astype(F32)
-        resid = resid - want[i % js, rr, part].astype(F32)
-        tile[...] += jnp.sum((resid * resid).reshape(orow // 8, 8, hq), axis=0)
 
     def rows_at(m):
         return pl.ds(pl.multiple_of(m * orow, orow), orow)

time: 102 us -> 102 us (level)
  no operation moved by 1% of the time
where the time goes in v9:
time: 102 us; the launch traced here: 101 us
  Pallas kernels  99.2 us (97%)
    pallas_call x1, Pallas kernels, fused(): pl.pallas_call(functools.partial(layer, nd), out_shape=(jax.ShapeDtypeStr...  99.2 us

profile of v9, /device:TPU:0, one launch (start us, length us, event | category | flops | bytes accessed | tf_op | source)
XLA Modules:
  0.0 101.4 jit_solution(10254203189864953759)
XLA Ops:
  0.6 99.2 %shard_map.104 = (bf16[512,1024]{1,0:T(8,128)(2,1)S(1)}, f32[1,128]{1,0:T(1,128)S(1)}) custom-call(s32[4]{0:T(128)} %order_in.1, bf16[512,1024]{1,0:T(8,128)(2,1)} %bitcast.5, bf16[512,1024]{1,0:T(8,128)(2,1)} %bitcast.6, f32[1,4096]{1,0:T(1,128)} %bitcast.7, f32[1,128]{1,0:T(1,128)} %constant.4.clone.freqs, bf16[512,512]{1,0:T(8,128)(2,1)} %w_query.1, ...), custom_call_target="tpu_custom_call" | custom-call | tf_op jit(solution)/shard_map/pallas_call | solution.py:894
  99.9 0.6 reduce_sum.9
  100.5 1.0 copy.12
